TPU v7x, 16 devices: a 4x2x1 block of a 4x4x8 slice. The times are simulated.
16 devices in a mesh: dp: 4 (over y, z, core), tp: 4 (over x).
Axes of the slice: x: 4, y: 2, z: 1, core: 2. Of those that a mesh axis runs over, the one named last changes fastest.
The devices are a block of a 4x4x8 slice.
Arguments:
- x: bfloat16 [4096, 4096], P(('dp', 'tp')), parts along dimension 0
- w_gate: bfloat16 [4096, 10240], P(None, 'tp')
- w_up: bfloat16 [4096, 10240], P(None, 'tp')
- w_down: bfloat16 [10240, 4096], P('tp')
Outputs:
- output: bfloat16 [4096, 4096], P(('dp', 'tp')), parts along dimension 0
There are 4 independent parts. A program takes and returns all parts, laid end to end along the dimension named above; an argument that names none is the same for every part.
All inputs are finite; a program needn't handle non-finite values.
Results may differ from a plain program's by a relative error of at most 0.016.
Values are sent between devices in bfloat16 or wider.
A program may use at most 768 MiB of HBM per device.

v0:
```python
import jax
import jax.numpy as jnp
from jax import lax
from jax.sharding import PartitionSpec as P


def solution(mesh):
    def step(x, w_gate, w_up, w_down):
        rows = lax.all_gather(x, "tp", axis=0, tiled=True)
        gate = jnp.dot(rows, w_gate, preferred_element_type=jnp.float32)
        up = jnp.dot(rows, w_up, preferred_element_type=jnp.float32)
        hidden = (jax.nn.gelu(gate) * up).astype(jnp.bfloat16)
        term = jnp.dot(hidden, w_down, preferred_element_type=jnp.float32).astype(jnp.bfloat16)
        return lax.psum_scatter(term, "tp", scatter_dimension=0, tiled=True)

    return jax.shard_map(
        step,
        mesh=mesh,
        in_specs=(P(("dp", "tp"), None), P(None, "tp"), P(None, "tp"), P("tp", None)),
        out_specs=P(("dp", "tp"), None),
        check_vma=False,
    )
```

profile of v0, /device:TPU:112, one launch (start us, length us, event | category | flops | bytes accessed | tf_op | source)
XLA Modules:
  0.0 257.8 jit_solution(17576330099739580156)
XLA Ops:
  6.5 0.0 all-gather.2.cloned.1.call-start
  6.6 0.7 all-gather.2.cloned.1.call-update
  7.3 0.1 reduce-scatter.2.cloned.1.call-start
  7.4 83.7 %all-gather.2.cloned.1.call-done = bf16[1024,4096]{1,0:T(8,128)(2,1)} async-done(((bf16[256,4096]{1,0:T(8,128)(2,1)}), bf16[1024,4096]{1,0:T(8,128)(2,1)}) %all-gather.2.cloned.1.call-update) | async-done | bytes 8388624 | tf_op jit(solution)/shard_map/all_gather | solution.py:9
  91.0 0.0 slice-start
  91.0 0.0 slice-start.1
  91.0 28.6 %fusion.9 = f32[1024,2560]{1,0:T(8,128)} fusion(bf16[1024,4096]{1,0:T(8,128)(2,1)} %all-gather.2.cloned.1.call-done, bf16[4096,2560]{1,0:T(8,128)(2,1)} %param.5), kind=kOutput, calls=%fused_computation.11 | convolution fusion | flops 21474836480 | bytes 39845888 | tf_op jit(solution)/shard_map/dot_general | solution.py:10
  119.7 0.0 slice-start.2
  119.7 0.0 slice-start.3
  119.7 0.0 slice-start.4
  119.7 29.8 %fusion.8 = bf16[1024,2560]{1,0:T(8,128)(2,1)S(1)} fusion(f32[1024,2560]{1,0:T(8,128)} %fusion.9, bf16[1024,4096]{1,0:T(8,128)(2,1)} %all-gather.2.cloned.1.call-done, bf16[4096,2560]{1,0:T(8,128)(2,1)} %param.6), kind=kOutput, calls=%fused_computation.9 | convolution fusion | flops 21501050880 | bytes 45088768 | tf_op jit(solution)/shard_map/dot_general | solution.py:11
  149.5 0.0 slice-done
  149.5 0.0 slice-done.1
  149.6 0.0 slice-done.2
  149.6 0.0 slice-done.3
  149.6 0.0 slice-done.4
  149.6 23.7 %convolution_convert_fusion = bf16[1024,4096]{1,0:T(8,128)(2,1)} fusion(bf16[1024,2560]{1,0:T(8,128)(2,1)S(1)} %fusion.8, bf16[2560,4096]{1,0:T(8,128)(2,1)S(1)} %bitcast.7), kind=kOutput, calls=%fused_computation.10 | convolution fusion | flops 21479030784 | bytes 34603008 | tf_op jit(solution)/shard_map/dot_general | solution.py:13
  173.3 0.1 reduce-scatter.2.cloned.1.call-update
  173.4 77.5 %reduce-scatter.2.cloned.1.call-done = bf16[256,4096]{1,0:T(8,128)(2,1)} async-done(((bf16[1024,4096]{1,0:T(8,128)(2,1)}), bf16[256,4096]{1,0:T(8,128)(2,1)}) %reduce-scatter.2.cloned.1.call-update) | async-done | bytes 2097168 | tf_op jit(solution)/shard_map/reduce_scatter | solution.py:14
  (1 shorter events, 0.0 us)
Async XLA Ops:
  6.5 84.5 %all-gather.2.cloned.1.call-start = ((), (), s32[]{:S(2)}) async-start(), calls=%async_computation.1 | async-start | bytes 10485760 | tf_op jit(solution)/shard_map/all_gather | solution.py:9
  7.3 243.6 %reduce-scatter.2.cloned.1.call-start = ((), (), s32[]{:S(2)}) async-start(), calls=%async_computation.2 | async-start | bytes 10485760 | tf_op jit(solution)/shard_map/reduce_scatter | solution.py:14
  91.0 58.5 %slice-start = ((s8[20971520]{0:T(1024)(128)(4,1)}), s8[4194304]{0:T(1024)(128)(4,1)S(1)}, s32[]{:S(2)}) async-start(s8[20971520]{0:T(1024)(128)(4,1)} %bitcast.6), calls=%async_computation.3 | async-start | bytes 8388608
  91.0 58.5 %slice-start.1 = ((s8[20971520]{0:T(1024)(128)(4,1)}), s8[4194304]{0:T(1024)(128)(4,1)S(1)}, s32[]{:S(2)}) async-start(s8[20971520]{0:T(1024)(128)(4,1)} %bitcast.6), calls=%async_computation.4 | async-start | bytes 8388608
  119.7 29.9 %slice-start.2 = ((s8[20971520]{0:T(1024)(128)(4,1)}), s8[4194304]{0:T(1024)(128)(4,1)S(1)}, s32[]{:S(2)}) async-start(s8[20971520]{0:T(1024)(128)(4,1)} %bitcast.6), calls=%async_computation.5 | async-start | bytes 8388608
  119.7 29.9 %slice-start.3 = ((s8[20971520]{0:T(1024)(128)(4,1)}), s8[4194304]{0:T(1024)(128)(4,1)S(1)}, s32[]{:S(2)}) async-start(s8[20971520]{0:T(1024)(128)(4,1)} %bitcast.6), calls=%async_computation.6 | async-start | bytes 8388608
  119.7 29.9 %slice-start.4 = ((s8[20971520]{0:T(1024)(128)(4,1)}), s8[4194304]{0:T(1024)(128)(4,1)S(1)}, s32[]{:S(2)}) async-start(s8[20971520]{0:T(1024)(128)(4,1)} %bitcast.6), calls=%async_computation.7 | async-start | bytes 8388608
Sparse Core Ops, SparseCore 0:
  8.9 82.1 all-gather.1
  173.5 77.3 reduce-scatter.1
where the time goes:
time: 258 us
  waiting for transfers between devices  162 us (63%)
  matrix products  82.2 us (32%)
  between operations  13.5 us (5%)
    all_gather x1, waiting for transfers between devices, step(): rows = lax.all_gather(x, 'tp', axis=0, tiled=True)  83.7 us
    reduce_scatter x1, waiting for transfers between devices, step(): return lax.psum_scatter(term, 'tp', scatter_dimension=0, tiled=True)  77.5 us
    dot_general x1, matrix products, step(): up = jnp.dot(rows, w_up, preferred_element_type=jnp.float32)  29.8 us
    dot_general x1, matrix products, step(): gate = jnp.dot(rows, w_gate, preferred_element_type=jnp.float32)  28.6 us
    dot_general x1, matrix products, step(): jnp.dot(hidden, w_down, preferred_element_type=jnp.float32)  23.7 us
  transfers between devices with their start and end apart: 2, of which 2 were waited for; matrix products, arithmetic and copies ran while one was open for 0% of the time, Pallas kernels for 0%

commit v1 on v0

v1 whole, which is shorter than its diff:
```python
import functools

import jax
import jax.numpy as jnp
from jax import lax
from jax.experimental import pallas as pl
from jax.experimental.pallas import tpu as pltpu
from jax.sharding import PartitionSpec as P

MESH = pl.DeviceIdType.MESH
F32 = jnp.float32
BF16 = jnp.bfloat16

TILE_H = 256
TILE_D = 512
SLOTS_H = 3
SLOTS_D = 3

OWN, FIRST, SECOND, FAR = range(4)


def kernel(
    n,
    x_ref, wg_ref, wu_ref, wd_ref, y_ref,
    xs, hid, wg, wu, wd, own, mid, to_dir, to_far, to_mrg, by_dir, by_far, by_mrg, out,
    x_sem, wg_sem, wu_sem, wd_sem, ag_send, ag_recv, dir_send, dir_recv, far_send, far_recv, mrg_send, mrg_recv, out_sem,
):
    me = lax.axis_index("tp")
    right, left = lax.rem(me + 1, n), lax.rem(me + n - 1, n)
    rows, d = x_ref.shape
    half = rows // 2
    n_h = wg_ref.shape[1] // TILE_H
    n_d = d // TILE_D
    passes = xs.shape[0]
    a, b = pl.ds(0, half), pl.ds(half, half)

    def load_h(g):
        col = pl.ds(pl.multiple_of(lax.rem(g, n_h) * TILE_H, TILE_H), TILE_H)
        s = lax.rem(g, SLOTS_H)
        return (
            pltpu.make_async_copy(wg_ref.at[:, col], wg.at[s], wg_sem.at[s]),
            pltpu.make_async_copy(wu_ref.at[:, col], wu.at[s], wu_sem.at[s]),
        )

    def load_d(g):
        col = pl.ds(pl.multiple_of(lax.rem(g, n_d) * TILE_D, TILE_D), TILE_D)
        s = lax.rem(g, SLOTS_D)
        return pltpu.make_async_copy(wd_ref.at[:, col], wd.at[s], wd_sem.at[s])

    def send(src, dst, send_sem, recv_sem, to):
        return pltpu.make_async_remote_copy(
            src_ref=src, dst_ref=dst, send_sem=send_sem, recv_sem=recv_sem, device_id={"tp": to}, device_id_type=MESH
        )

    own_x = pltpu.make_async_copy(x_ref, xs.at[OWN], x_sem)
    own_x.start()
    for g in range(SLOTS_H):
        for copy in load_h(g):
            copy.start()
    for g in range(SLOTS_D):
        load_d(g).start()

    barrier = pltpu.get_barrier_semaphore()
    for neighbour in (left, right):
        pl.semaphore_signal(barrier, inc=1, device_id={"tp": neighbour}, device_id_type=MESH)
    pl.semaphore_wait(barrier, 2)
    own_x.wait()

    gather = [
        send(xs.at[OWN, a], xs.at[FIRST, a], ag_send.at[0], ag_recv.at[0], right),
        send(xs.at[OWN, b], xs.at[FIRST, b], ag_send.at[1], ag_recv.at[1], left),
        send(xs.at[OWN, b], xs.at[SECOND, a], ag_send.at[2], ag_recv.at[2], right),
        send(xs.at[OWN, a], xs.at[SECOND, b], ag_send.at[3], ag_recv.at[3], left),
        send(xs.at[FIRST, a], xs.at[FAR, a], ag_send.at[4], ag_recv.at[4], right),
        send(xs.at[FIRST, b], xs.at[FAR, b], ag_send.at[5], ag_recv.at[5], left),
    ]
    direct = [
        send(to_dir.at[:, b], by_dir.at[:, b], dir_send.at[0], dir_recv.at[0], right),
        send(to_dir.at[:, a], by_dir.at[:, a], dir_send.at[1], dir_recv.at[1], left),
    ]

    def far(j):
        return (
            send(to_far.at[j, a], by_far.at[j, b], far_send.at[j, 0], far_recv.at[j, 0], right),
            send(to_far.at[j, b], by_far.at[j, a], far_send.at[j, 1], far_recv.at[j, 1], left),
        )

    def merged(j):
        return (
            send(to_mrg.at[j, b], by_mrg.at[j, a], mrg_send.at[j, 0], mrg_recv.at[j, 0], right),
            send(to_mrg.at[j, a], by_mrg.at[j, b], mrg_send.at[j, 1], mrg_recv.at[j, 1], left),
        )

    for copy in gather[:4]:
        copy.start()

    def hidden(p):
        @pl.loop(0, n_h)
        def _(i):
            g = p * n_h + i
            s = lax.rem(g, SLOTS_H)
            for copy in load_h(g):
                copy.wait()
            gate = jnp.dot(xs[p], wg[s], preferred_element_type=F32)
            up = jnp.dot(xs[p], wu[s], preferred_element_type=F32)
            col = pl.ds(pl.multiple_of(i * TILE_H, TILE_H), TILE_H)
            hid[:, col] = (jax.nn.gelu(gate) * up).astype(BF16)

            @pl.when(g + SLOTS_H < passes * n_h)
            def _():
                for copy in load_h(g + SLOTS_H):
                    copy.start()

    def down(p, put):
        @pl.loop(0, n_d)
        def _(j):
            g = p * n_d + j
            s = lax.rem(g, SLOTS_D)
            load_d(g).wait()
            put(j, jnp.dot(hid[...], wd[s], preferred_element_type=F32))

            @pl.when(g + SLOTS_D < passes * n_d)
            def _():
                load_d(g + SLOTS_D).start()

    def put_own(j, term):
        own[j] = term

    def put_direct(j, term):
        to_dir[j] = term.astype(BF16)

    def put_mid(j, term):
        mid[j] = term

    def put_far(j, term):
        to_far[j] = term.astype(BF16)
        for copy in far(j):
            copy.start()

    hidden(OWN)
    down(OWN, put_own)

    for got, onward in zip(gather[0:2], gather[4:6]):
        got.wait_recv()
        onward.start()
    hidden(FIRST)
    down(FIRST, put_direct)
    for copy in direct:
        copy.start()

    for got in gather[2:4]:
        got.wait_recv()
    hidden(SECOND)
    down(SECOND, put_mid)

    for got in gather[4:6]:
        got.wait_recv()
    hidden(FAR)
    down(FAR, put_far)

    @pl.loop(0, n_d)
    def _(j):
        for copy in far(j):
            copy.wait_recv()
        to_mrg[j] = (mid[j] + by_far[j].astype(F32)).astype(BF16)
        for copy in merged(j):
            copy.start()

    for copy in direct:
        copy.wait_recv()

    def write(j):
        col = pl.ds(pl.multiple_of(j * TILE_D, TILE_D), TILE_D)
        return pltpu.make_async_copy(out.at[j], y_ref.at[:, col], out_sem.at[j])

    @pl.loop(0, n_d)
    def _(j):
        for copy in merged(j):
            copy.wait_recv()
        out[j] = (own[j] + by_dir[j].astype(F32) + by_mrg[j].astype(F32)).astype(BF16)
        write(j).start()

    for copy in gather + direct:
        copy.wait_send()

    @pl.loop(0, n_d)
    def _(j):
        for copy in far(j) + merged(j):
            copy.wait_send()
        write(j).wait()


def solution(mesh):
    n = mesh.shape["tp"]

    def step(x, w_gate, w_up, w_down):
        rows, d = x.shape
        ff = w_gate.shape[1]
        n_d = d // TILE_D
        dma = pltpu.SemaphoreType.DMA
        pieces = (n_d, rows, TILE_D)
        return pl.pallas_call(
            functools.partial(kernel, n),
            out_shape=jax.ShapeDtypeStruct((rows, d), BF16),
            in_specs=[pl.BlockSpec(memory_space=pl.ANY)] * 4,
            out_specs=pl.BlockSpec(memory_space=pl.ANY),
            scratch_shapes=[
                pltpu.VMEM((n, rows, d), BF16),
                pltpu.VMEM((rows, ff), BF16),
                pltpu.VMEM((SLOTS_H, d, TILE_H), BF16),
                pltpu.VMEM((SLOTS_H, d, TILE_H), BF16),
                pltpu.VMEM((SLOTS_D, ff, TILE_D), BF16),
                pltpu.VMEM(pieces, F32),
                pltpu.VMEM(pieces, F32),
                pltpu.VMEM(pieces, BF16),
                pltpu.VMEM(pieces, BF16),
                pltpu.VMEM(pieces, BF16),
                pltpu.VMEM(pieces, BF16),
                pltpu.VMEM(pieces, BF16),
                pltpu.VMEM(pieces, BF16),
                pltpu.VMEM(pieces, BF16),
                dma, dma((SLOTS_H,)), dma((SLOTS_H,)), dma((SLOTS_D,)),
                dma((6,)), dma((6,)), dma((2,)), dma((2,)),
                dma((n_d, 2)), dma((n_d, 2)), dma((n_d, 2)), dma((n_d, 2)), dma((n_d,)),
            ],
            compiler_params=pltpu.CompilerParams(
                collective_id=0, has_side_effects=True, vmem_limit_bytes=63 * 1024 * 1024
            ),
            cost_estimate=pl.CostEstimate(
                flops=6 * n * rows * d * ff, bytes_accessed=6 * n * d * ff, transcendentals=n * rows * ff
            ),
            name="mlp_ring",
        )(x, w_gate, w_up, w_down)

    return jax.shard_map(
        step,
        mesh=mesh,
        in_specs=(P(("dp", "tp"), None), P(None, "tp"), P(None, "tp"), P("tp", None)),
        out_specs=P(("dp", "tp"), None),
        check_vma=False,
    )
```

time: 258 us -> 150 us (0.58)
  waiting for transfers between devices: 162 us -> 0 us
  Pallas kernels: 0 us -> 147 us
  matrix products: 82.2 us -> 0 us
  between operations: 13.5 us -> 0.01 us
  local copies, waits for them, and re-layouts: 0.02 us -> 3.13 us
    pallas_call x0 -> x1, Pallas kernels: none -> 147 us  [step(): pl.pallas_call(functools.partial(kernel, n), out_shape=jax.ShapeDtypeStru...]
    all_gather x1 -> x0, waiting for transfers between devices: 83.7 us -> none  [step(): rows = lax.all_gather(x, 'tp', axis=0, tiled=True)]
    dot_general x3 -> x0, matrix products: 82.2 us -> none  [the longest x1 29.8 us: step(): up = jnp.dot(rows, w_up, preferred_element_type=jnp.float32)]
    reduce_scatter x1 -> x0, waiting for transfers between devices: 77.5 us -> none  [step(): return lax.psum_scatter(term, 'tp', scatter_dimension=0, tiled=True)]
    unnamed x10 -> x1, local copies, waits for them, and re-layouts: 0.02 us -> 3.13 us
  transfers between devices with their start and end apart: 2 -> 0, of which waited for: 2 -> 0; matrix products, arithmetic and copies ran while one was open for 0% -> 0% of each run, Pallas kernels for 0% -> 0%
where the time goes in v1:
time: 150 us
  Pallas kernels  147 us (98%)
  local copies, waits for them, and re-layouts  3.13 us (2%)
    pallas_call x1, Pallas kernels, step(): pl.pallas_call(functools.partial(kernel, n), out_shape=jax.ShapeDtypeStru...  147 us
    unnamed x1, local copies, waits for them, and re-layouts  3.13 us

profile of v1, /device:TPU:112, one launch (start us, length us, event | category | flops | bytes accessed | tf_op | source)
XLA Modules:
  0.0 150.0 jit_solution(7591234304039566051)
XLA Ops:
  0.0 146.8 %mlp_ring.1 = bf16[256,4096]{1,0:T(8,128)(2,1)} custom-call(bf16[256,4096]{1,0:T(8,128)(2,1)} %x_ref.1, bf16[4096,2560]{1,0:T(8,128)(2,1)} %wg_ref.1, bf16[4096,2560]{1,0:T(8,128)(2,1)} %wu_ref.1, bf16[2560,4096]{1,0:T(8,128)(2,1)} %wd_ref.1), custom_call_target="tpu_custom_call" | custom-call | flops 64424509440 | bytes 251658240 | tf_op jit(solution)/shard_map/mlp_ring/pallas_call | solution.py:202
  146.8 3.1 %copy.6 = bf16[256,4096]{1,0:T(8,128)(2,1)} copy(bf16[256,4096]{1,0:T(8,128)(2,1)} %mlp_ring.1) | data formatting | bytes 4194304

commit v2 on v1

--- a/solution.py
+++ b/solution.py
@@ -15,6 +15,7 @@
 TILE_D = 512
 SLOTS_H = 3
 SLOTS_D = 3
+VMEM_MIB = 54
 
 OWN, FIRST, SECOND, FAR = range(4)
 
@@ -22,8 +23,8 @@
 def kernel(
     n,
     x_ref, wg_ref, wu_ref, wd_ref, y_ref,
-    xs, hid, wg, wu, wd, own, mid, to_dir, to_far, to_mrg, by_dir, by_far, by_mrg, out,
-    x_sem, wg_sem, wu_sem, wd_sem, ag_send, ag_recv, dir_send, dir_recv, far_send, far_recv, mrg_send, mrg_recv, out_sem,
+    xs, hid, wg, wu, wd, own, mid, to_dir, to_far, to_mrg, by_dir, by_far, by_mrg,
+    x_sem, wg_sem, wu_sem, wd_sem, ag_send, ag_recv, dir_send, dir_recv, far_send, far_recv, mrg_send, mrg_recv,
 ):
     me = lax.axis_index("tp")
     right, left = lax.rem(me + 1, n), lax.rem(me + n - 1, n)
@@ -169,16 +170,12 @@
     for copy in direct:
         copy.wait_recv()
 
-    def write(j):
-        col = pl.ds(pl.multiple_of(j * TILE_D, TILE_D), TILE_D)
-        return pltpu.make_async_copy(out.at[j], y_ref.at[:, col], out_sem.at[j])
-
     @pl.loop(0, n_d)
     def _(j):
         for copy in merged(j):
             copy.wait_recv()
-        out[j] = (own[j] + by_dir[j].astype(F32) + by_mrg[j].astype(F32)).astype(BF16)
-        write(j).start()
+        col = pl.ds(pl.multiple_of(j * TILE_D, TILE_D), TILE_D)
+        y_ref[:, col] = (own[j] + by_dir[j].astype(F32) + by_mrg[j].astype(F32)).astype(BF16)
 
     for copy in gather + direct:
         copy.wait_send()
@@ -187,7 +184,6 @@
     def _(j):
         for copy in far(j) + merged(j):
             copy.wait_send()
-        write(j).wait()
 
 
 def solution(mesh):
@@ -201,9 +197,9 @@
         pieces = (n_d, rows, TILE_D)
         return pl.pallas_call(
             functools.partial(kernel, n),
-            out_shape=jax.ShapeDtypeStruct((rows, d), BF16),
+            out_shape=pltpu.VMEM((rows, d), BF16),
             in_specs=[pl.BlockSpec(memory_space=pl.ANY)] * 4,
-            out_specs=pl.BlockSpec(memory_space=pl.ANY),
+            out_specs=pl.BlockSpec(memory_space=pltpu.VMEM),
             scratch_shapes=[
                 pltpu.VMEM((n, rows, d), BF16),
                 pltpu.VMEM((rows, ff), BF16),
@@ -218,13 +214,12 @@
                 pltpu.VMEM(pieces, BF16),
                 pltpu.VMEM(pieces, BF16),
                 pltpu.VMEM(pieces, BF16),
-                pltpu.VMEM(pieces, BF16),
                 dma, dma((SLOTS_H,)), dma((SLOTS_H,)), dma((SLOTS_D,)),
                 dma((6,)), dma((6,)), dma((2,)), dma((2,)),
-                dma((n_d, 2)), dma((n_d, 2)), dma((n_d, 2)), dma((n_d, 2)), dma((n_d,)),
+                dma((n_d, 2)), dma((n_d, 2)), dma((n_d, 2)), dma((n_d, 2)),
             ],
             compiler_params=pltpu.CompilerParams(
-                collective_id=0, has_side_effects=True, vmem_limit_bytes=63 * 1024 * 1024
+                collective_id=0, has_side_effects=True, vmem_limit_bytes=VMEM_MIB * 1024 * 1024
             ),
             cost_estimate=pl.CostEstimate(
                 flops=6 * n * rows * d * ff, bytes_accessed=6 * n * d * ff, transcendentals=n * rows * ff

time: 150 us -> 148 us (0.987)
  local copies, waits for them, and re-layouts: 3.13 us -> 1.32 us
    unnamed x1, local copies, waits for them, and re-layouts: 3.13 us -> 1.32 us
where the time goes in v2:
time: 148 us; the launch traced here: 147 us
  Pallas kernels  146 us (99%)
    pallas_call x1, Pallas kernels, step(): pl.pallas_call(functools.partial(kernel, n), out_shape=pltpu.VMEM((rows,...  146 us

profile of v2, /device:TPU:112, one launch (start us, length us, event | category | flops | bytes accessed | tf_op | source)
XLA Modules:
  0.0 147.4 jit_solution(12305198838452429215)
XLA Ops:
  0.0 146.1 %mlp_ring.1 = bf16[256,4096]{1,0:T(8,128)(2,1)S(1)} custom-call(bf16[256,4096]{1,0:T(8,128)(2,1)} %x_ref.1, bf16[4096,2560]{1,0:T(8,128)(2,1)} %wg_ref.1, bf16[4096,2560]{1,0:T(8,128)(2,1)} %wu_ref.1, bf16[2560,4096]{1,0:T(8,128)(2,1)} %wd_ref.1), custom_call_target="tpu_custom_call" | custom-call | flops 64424509440 | bytes 251658240 | tf_op jit(solution)/shard_map/mlp_ring/pallas_call | solution.py:198
  146.1 1.3 copy.6

commit v3 on v2

--- a/solution.py
+++ b/solution.py
@@ -53,19 +53,14 @@
             src_ref=src, dst_ref=dst, send_sem=send_sem, recv_sem=recv_sem, device_id={"tp": to}, device_id_type=MESH
         )
 
-    own_x = pltpu.make_async_copy(x_ref, xs.at[OWN], x_sem)
-    own_x.start()
-    for g in range(SLOTS_H):
-        for copy in load_h(g):
-            copy.start()
-    for g in range(SLOTS_D):
-        load_d(g).start()
+    own_x = [pltpu.make_async_copy(x_ref.at[h], xs.at[OWN, h], x_sem.at[k]) for k, h in enumerate((a, b))]
+    for copy in own_x:
+        copy.start()
 
     barrier = pltpu.get_barrier_semaphore()
     for neighbour in (left, right):
         pl.semaphore_signal(barrier, inc=1, device_id={"tp": neighbour}, device_id_type=MESH)
     pl.semaphore_wait(barrier, 2)
-    own_x.wait()
 
     gather = [
         send(xs.at[OWN, a], xs.at[FIRST, a], ag_send.at[0], ag_recv.at[0], right),
@@ -92,8 +87,17 @@
             send(to_mrg.at[j, a], by_mrg.at[j, b], mrg_send.at[j, 1], mrg_recv.at[j, 1], left),
         )
 
-    for copy in gather[:4]:
+    own_x[0].wait()
+    gather[0].start()
+    own_x[1].wait()
+    for copy in gather[1:4]:
         copy.start()
+
+    for g in range(SLOTS_H):
+        for copy in load_h(g):
+            copy.start()
+    for g in range(SLOTS_D):
+        load_d(g).start()
 
     def hidden(p):
         @pl.loop(0, n_h)
@@ -214,7 +218,7 @@
                 pltpu.VMEM(pieces, BF16),
                 pltpu.VMEM(pieces, BF16),
                 pltpu.VMEM(pieces, BF16),
-                dma, dma((SLOTS_H,)), dma((SLOTS_H,)), dma((SLOTS_D,)),
+                dma((2,)), dma((SLOTS_H,)), dma((SLOTS_H,)), dma((SLOTS_D,)),
                 dma((6,)), dma((6,)), dma((2,)), dma((2,)),
                 dma((n_d, 2)), dma((n_d, 2)), dma((n_d, 2)), dma((n_d, 2)),
             ],

time: 148 us -> 143 us (0.966)
  Pallas kernels: 146 us -> 142 us
    pallas_call x1, Pallas kernels: 146 us -> 142 us  [step(): pl.pallas_call(functools.partial(kernel, n), out_shape=pltpu.VMEM((rows,...]
where the time goes in v3:
time: 143 us
  Pallas kernels  142 us (99%)
    pallas_call x1, Pallas kernels, step(): pl.pallas_call(functools.partial(kernel, n), out_shape=pltpu.VMEM((rows,...  142 us

profile of v3, /device:TPU:112, one launch (start us, length us, event | category | flops | bytes accessed | tf_op | source)
XLA Modules:
  0.0 143.0 jit_solution(17600920055145331231)
XLA Ops:
  0.0 141.7 %mlp_ring.1 = bf16[256,4096]{1,0:T(8,128)(2,1)S(1)} custom-call(bf16[256,4096]{1,0:T(8,128)(2,1)} %x_ref.1, bf16[4096,2560]{1,0:T(8,128)(2,1)} %wg_ref.1, bf16[4096,2560]{1,0:T(8,128)(2,1)} %wu_ref.1, bf16[2560,4096]{1,0:T(8,128)(2,1)} %wd_ref.1), custom_call_target="tpu_custom_call" | custom-call | flops 64424509440 | bytes 251658240 | tf_op jit(solution)/shard_map/mlp_ring/pallas_call | solution.py:202
  141.7 1.3 copy.6

commit v4 on v3

--- a/solution.py
+++ b/solution.py
@@ -16,6 +16,7 @@
 SLOTS_H = 3
 SLOTS_D = 3
 VMEM_MIB = 54
+HEAD = 32
 
 OWN, FIRST, SECOND, FAR = range(4)
 
@@ -34,6 +35,8 @@
     n_d = d // TILE_D
     passes = xs.shape[0]
     a, b = pl.ds(0, half), pl.ds(half, half)
+    a0, a1 = pl.ds(0, HEAD), pl.ds(HEAD, half - HEAD)
+    b0, b1 = pl.ds(half, HEAD), pl.ds(half + HEAD, half - HEAD)
 
     def load_h(g):
         col = pl.ds(pl.multiple_of(lax.rem(g, n_h) * TILE_H, TILE_H), TILE_H)
@@ -53,22 +56,27 @@
             src_ref=src, dst_ref=dst, send_sem=send_sem, recv_sem=recv_sem, device_id={"tp": to}, device_id_type=MESH
         )
 
-    own_x = [pltpu.make_async_copy(x_ref.at[h], xs.at[OWN, h], x_sem.at[k]) for k, h in enumerate((a, b))]
-    for copy in own_x:
-        copy.start()
-
     barrier = pltpu.get_barrier_semaphore()
     for neighbour in (left, right):
         pl.semaphore_signal(barrier, inc=1, device_id={"tp": neighbour}, device_id_type=MESH)
+    own_x = [pltpu.make_async_copy(x_ref.at[r], xs.at[OWN, r], x_sem.at[k]) for k, r in enumerate((a0, b0, a1, b1))]
+    for copy in own_x:
+        copy.start()
     pl.semaphore_wait(barrier, 2)
 
-    gather = [
-        send(xs.at[OWN, a], xs.at[FIRST, a], ag_send.at[0], ag_recv.at[0], right),
-        send(xs.at[OWN, b], xs.at[FIRST, b], ag_send.at[1], ag_recv.at[1], left),
-        send(xs.at[OWN, b], xs.at[SECOND, a], ag_send.at[2], ag_recv.at[2], right),
-        send(xs.at[OWN, a], xs.at[SECOND, b], ag_send.at[3], ag_recv.at[3], left),
-        send(xs.at[FIRST, a], xs.at[FAR, a], ag_send.at[4], ag_recv.at[4], right),
-        send(xs.at[FIRST, b], xs.at[FAR, b], ag_send.at[5], ag_recv.at[5], left),
+    heads = [
+        send(xs.at[OWN, a0], xs.at[FIRST, a0], ag_send.at[0], ag_recv.at[0], right),
+        send(xs.at[OWN, b0], xs.at[FIRST, b0], ag_send.at[1], ag_recv.at[1], left),
+        send(xs.at[OWN, a1], xs.at[FIRST, a1], ag_send.at[2], ag_recv.at[2], right),
+        send(xs.at[OWN, b1], xs.at[FIRST, b1], ag_send.at[3], ag_recv.at[3], left),
+    ]
+    tails = [
+        send(xs.at[OWN, b], xs.at[SECOND, a], ag_send.at[4], ag_recv.at[4], right),
+        send(xs.at[OWN, a], xs.at[SECOND, b], ag_send.at[5], ag_recv.at[5], left),
+    ]
+    onward = [
+        send(xs.at[FIRST, a], xs.at[FAR, a], ag_send.at[6], ag_recv.at[6], right),
+        send(xs.at[FIRST, b], xs.at[FAR, b], ag_send.at[7], ag_recv.at[7], left),
     ]
     direct = [
         send(to_dir.at[:, b], by_dir.at[:, b], dir_send.at[0], dir_recv.at[0], right),
@@ -87,10 +95,10 @@
             send(to_mrg.at[j, a], by_mrg.at[j, b], mrg_send.at[j, 1], mrg_recv.at[j, 1], left),
         )
 
-    own_x[0].wait()
-    gather[0].start()
-    own_x[1].wait()
-    for copy in gather[1:4]:
+    for loaded, copy in zip(own_x, heads):
+        loaded.wait()
+        copy.start()
+    for copy in tails:
         copy.start()
 
     for g in range(SLOTS_H):
@@ -145,21 +153,22 @@
     hidden(OWN)
     down(OWN, put_own)
 
-    for got, onward in zip(gather[0:2], gather[4:6]):
-        got.wait_recv()
-        onward.start()
+    for copy in heads:
+        copy.wait_recv()
+    for copy in onward:
+        copy.start()
     hidden(FIRST)
     down(FIRST, put_direct)
     for copy in direct:
         copy.start()
 
-    for got in gather[2:4]:
-        got.wait_recv()
+    for copy in tails:
+        copy.wait_recv()
     hidden(SECOND)
     down(SECOND, put_mid)
 
-    for got in gather[4:6]:
-        got.wait_recv()
+    for copy in onward:
+        copy.wait_recv()
     hidden(FAR)
     down(FAR, put_far)
 
@@ -173,6 +182,13 @@
 
     for copy in direct:
         copy.wait_recv()
+    for copy in heads + tails + onward + direct:
+        copy.wait_send()
+
+    @pl.loop(0, n_d)
+    def _(j):
+        for copy in far(j):
+            copy.wait_send()
 
     @pl.loop(0, n_d)
     def _(j):
@@ -180,13 +196,7 @@
             copy.wait_recv()
         col = pl.ds(pl.multiple_of(j * TILE_D, TILE_D), TILE_D)
         y_ref[:, col] = (own[j] + by_dir[j].astype(F32) + by_mrg[j].astype(F32)).astype(BF16)
-
-    for copy in gather + direct:
-        copy.wait_send()
-
-    @pl.loop(0, n_d)
-    def _(j):
-        for copy in far(j) + merged(j):
+        for copy in merged(j):
             copy.wait_send()
 
 
@@ -218,8 +228,8 @@
                 pltpu.VMEM(pieces, BF16),
                 pltpu.VMEM(pieces, BF16),
                 pltpu.VMEM(pieces, BF16),
-                dma((2,)), dma((SLOTS_H,)), dma((SLOTS_H,)), dma((SLOTS_D,)),
-                dma((6,)), dma((6,)), dma((2,)), dma((2,)),
+                dma((4,)), dma((SLOTS_H,)), dma((SLOTS_H,)), dma((SLOTS_D,)),
+                dma((8,)), dma((8,)), dma((2,)), dma((2,)),
                 dma((n_d, 2)), dma((n_d, 2)), dma((n_d, 2)), dma((n_d, 2)),
             ],
             compiler_params=pltpu.CompilerParams(

time: 143 us -> 143 us (level)
  no operation moved by 1% of the time
where the time goes in v4:
time: 143 us
  Pallas kernels  141 us (99%)
    pallas_call x1, Pallas kernels, step(): pl.pallas_call(functools.partial(kernel, n), out_shape=pltpu.VMEM((rows,...  141 us

profile of v4, /device:TPU:112, one launch (start us, length us, event | category | flops | bytes accessed | tf_op | source)
XLA Modules:
  0.0 142.7 jit_solution(7212399955521313560)
XLA Ops:
  0.0 141.4 %mlp_ring.1 = bf16[256,4096]{1,0:T(8,128)(2,1)S(1)} custom-call(bf16[256,4096]{1,0:T(8,128)(2,1)} %x_ref.1, bf16[4096,2560]{1,0:T(8,128)(2,1)} %wg_ref.1, bf16[4096,2560]{1,0:T(8,128)(2,1)} %wu_ref.1, bf16[2560,4096]{1,0:T(8,128)(2,1)} %wd_ref.1), custom_call_target="tpu_custom_call" | custom-call | flops 64424509440 | bytes 251658240 | tf_op jit(solution)/shard_map/mlp_ring/pallas_call | solution.py:212
  141.4 1.3 copy.6

commit v5 on v4

--- a/solution.py
+++ b/solution.py
@@ -65,8 +65,8 @@
     pl.semaphore_wait(barrier, 2)
 
     heads = [
-        send(xs.at[OWN, a0], xs.at[FIRST, a0], ag_send.at[0], ag_recv.at[0], right),
-        send(xs.at[OWN, b0], xs.at[FIRST, b0], ag_send.at[1], ag_recv.at[1], left),
+        send(x_ref.at[a0], xs.at[FIRST, a0], ag_send.at[0], ag_recv.at[0], right),
+        send(x_ref.at[b0], xs.at[FIRST, b0], ag_send.at[1], ag_recv.at[1], left),
         send(xs.at[OWN, a1], xs.at[FIRST, a1], ag_send.at[2], ag_recv.at[2], right),
         send(xs.at[OWN, b1], xs.at[FIRST, b1], ag_send.at[3], ag_recv.at[3], left),
     ]
@@ -95,8 +95,11 @@
             send(to_mrg.at[j, a], by_mrg.at[j, b], mrg_send.at[j, 1], mrg_recv.at[j, 1], left),
         )
 
-    for loaded, copy in zip(own_x, heads):
-        loaded.wait()
+    for copy in heads[:2]:
+        copy.start()
+    for copy in own_x:
+        copy.wait()
+    for copy in heads[2:]:
         copy.start()
     for copy in tails:
         copy.start()

time: 143 us -> 142 us (level)
  no operation moved by 1% of the time
where the time goes in v5:
time: 142 us
  Pallas kernels  141 us (99%)
    pallas_call x1, Pallas kernels, step(): pl.pallas_call(functools.partial(kernel, n), out_shape=pltpu.VMEM((rows,...  141 us

profile of v5, /device:TPU:112, one launch (start us, length us, event | category | flops | bytes accessed | tf_op | source)
XLA Modules:
  0.0 142.2 jit_solution(16358974518440615106)
XLA Ops:
  0.0 140.8 %mlp_ring.1 = bf16[256,4096]{1,0:T(8,128)(2,1)S(1)} custom-call(bf16[256,4096]{1,0:T(8,128)(2,1)} %x_ref.1, bf16[4096,2560]{1,0:T(8,128)(2,1)} %wg_ref.1, bf16[4096,2560]{1,0:T(8,128)(2,1)} %wu_ref.1, bf16[2560,4096]{1,0:T(8,128)(2,1)} %wd_ref.1), custom_call_target="tpu_custom_call" | custom-call | flops 64424509440 | bytes 251658240 | tf_op jit(solution)/shard_map/mlp_ring/pallas_call | solution.py:215
  140.8 1.3 copy.6

commit v6 on v5

--- a/solution.py
+++ b/solution.py
@@ -15,7 +15,8 @@
 TILE_D = 512
 SLOTS_H = 3
 SLOTS_D = 3
-VMEM_MIB = 54
+VMEM_MIB = 46
+FINISH_MIB = 4
 HEAD = 32
 
 OWN, FIRST, SECOND, FAR = range(4)
@@ -23,8 +24,8 @@
 
 def kernel(
     n,
-    x_ref, wg_ref, wu_ref, wd_ref, y_ref,
-    xs, hid, wg, wu, wd, own, mid, to_dir, to_far, to_mrg, by_dir, by_far, by_mrg,
+    x_ref, wg_ref, wu_ref, wd_ref, y_ref, own, by_mrg,
+    xs, hid, wg, wu, wd, mid, to_dir, to_far, to_mrg, by_dir, by_far,
     x_sem, wg_sem, wu_sem, wd_sem, ag_send, ag_recv, dir_send, dir_recv, far_send, far_recv, mrg_send, mrg_recv,
 ):
     me = lax.axis_index("tp")
@@ -193,7 +194,10 @@
         for copy in far(j):
             copy.wait_send()
 
-    @pl.loop(0, n_d)
+    last = n_d - 1
+    own[last] += by_dir[last].astype(F32)
+
+    @pl.loop(0, last)
     def _(j):
         for copy in merged(j):
             copy.wait_recv()
@@ -202,6 +206,23 @@
         for copy in merged(j):
             copy.wait_send()
 
+    for copy in merged(last):
+        copy.wait_recv()
+    for copy in merged(last):
+        copy.wait_send()
+
+
+def finish(y_ref, own, by_mrg, out_ref, piece, sem):
+    last = own.shape[0] - 1
+    done = pl.ds(0, last * TILE_D)
+    rest = pltpu.make_async_copy(y_ref.at[:, done], out_ref.at[:, done], sem.at[0])
+    rest.start()
+    piece[...] = (own[last] + by_mrg[last].astype(F32)).astype(BF16)
+    end = pltpu.make_async_copy(piece, out_ref.at[:, pl.ds(last * TILE_D, TILE_D)], sem.at[1])
+    end.start()
+    rest.wait()
+    end.wait()
+
 
 def solution(mesh):
     n = mesh.shape["tp"]
@@ -212,11 +233,12 @@
         n_d = d // TILE_D
         dma = pltpu.SemaphoreType.DMA
         pieces = (n_d, rows, TILE_D)
-        return pl.pallas_call(
+        vmem = pl.BlockSpec(memory_space=pltpu.VMEM)
+        parts = pl.pallas_call(
             functools.partial(kernel, n),
-            out_shape=pltpu.VMEM((rows, d), BF16),
+            out_shape=(pltpu.VMEM((rows, d), BF16), pltpu.VMEM(pieces, F32), pltpu.VMEM(pieces, BF16)),
             in_specs=[pl.BlockSpec(memory_space=pl.ANY)] * 4,
-            out_specs=pl.BlockSpec(memory_space=pltpu.VMEM),
+            out_specs=(vmem, vmem, vmem),
             scratch_shapes=[
                 pltpu.VMEM((n, rows, d), BF16),
                 pltpu.VMEM((rows, ff), BF16),
@@ -224,8 +246,6 @@
                 pltpu.VMEM((SLOTS_H, d, TILE_H), BF16),
                 pltpu.VMEM((SLOTS_D, ff, TILE_D), BF16),
                 pltpu.VMEM(pieces, F32),
-                pltpu.VMEM(pieces, F32),
-                pltpu.VMEM(pieces, BF16),
                 pltpu.VMEM(pieces, BF16),
                 pltpu.VMEM(pieces, BF16),
                 pltpu.VMEM(pieces, BF16),
@@ -243,6 +263,15 @@
             ),
             name="mlp_ring",
         )(x, w_gate, w_up, w_down)
+        return pl.pallas_call(
+            finish,
+            out_shape=jax.ShapeDtypeStruct((rows, d), BF16),
+            in_specs=[vmem] * 3,
+            out_specs=pl.BlockSpec(memory_space=pl.ANY),
+            scratch_shapes=[pltpu.VMEM((rows, TILE_D), BF16), dma((2,))],
+            compiler_params=pltpu.CompilerParams(vmem_limit_bytes=FINISH_MIB * 1024 * 1024),
+            name="finish",
+        )(*parts)
 
     return jax.shard_map(
         step,

time: 142 us -> 142 us (level)
    pallas_call x1 -> x2, Pallas kernels: 141 us -> 142 us  [the longest x1 141 us: step(): pl.pallas_call(functools.partial(kernel, n), out_shape=(pltpu.VMEM((rows,...]
where the time goes in v6:
time: 142 us
  Pallas kernels  142 us (100%)
    pallas_call x1, Pallas kernels, step(): pl.pallas_call(functools.partial(kernel, n), out_shape=(pltpu.VMEM((rows,...  141 us

profile of v6, /device:TPU:112, one launch (start us, length us, event | category | flops | bytes accessed | tf_op | source)
XLA Modules:
  0.0 142.1 jit_solution(7592816752178659922)
XLA Ops:
  0.0 140.7 %mlp_ring.1 = (bf16[256,4096]{1,0:T(8,128)(2,1)S(1)}, f32[8,256,512]{2,1,0:T(8,128)S(1)}, bf16[8,256,512]{2,1,0:T(8,128)(2,1)S(1)}) custom-call(bf16[256,4096]{1,0:T(8,128)(2,1)} %x_ref.1, bf16[4096,2560]{1,0:T(8,128)(2,1)} %wg_ref.1, bf16[4096,2560]{1,0:T(8,128)(2,1)} %wu_ref.1, bf16[2560,4096]{1,0:T(8,128)(2,1)} %wd_ref.1), custom_call_target="tpu_custom_call" | custom-call | flops 64424509440 | bytes 251658240 | tf_op jit(solution)/shard_map/mlp_ring/pallas_call | solution.py:237
  140.8 1.3 finish.1

commit v7 on v6

--- a/solution.py
+++ b/solution.py
@@ -17,7 +17,6 @@
 SLOTS_D = 3
 VMEM_MIB = 46
 FINISH_MIB = 4
-HEAD = 32
 
 OWN, FIRST, SECOND, FAR = range(4)
 
@@ -36,8 +35,6 @@
     n_d = d // TILE_D
     passes = xs.shape[0]
     a, b = pl.ds(0, half), pl.ds(half, half)
-    a0, a1 = pl.ds(0, HEAD), pl.ds(HEAD, half - HEAD)
-    b0, b1 = pl.ds(half, HEAD), pl.ds(half + HEAD, half - HEAD)
 
     def load_h(g):
         col = pl.ds(pl.multiple_of(lax.rem(g, n_h) * TILE_H, TILE_H), TILE_H)
@@ -60,24 +57,21 @@
     barrier = pltpu.get_barrier_semaphore()
     for neighbour in (left, right):
         pl.semaphore_signal(barrier, inc=1, device_id={"tp": neighbour}, device_id_type=MESH)
-    own_x = [pltpu.make_async_copy(x_ref.at[r], xs.at[OWN, r], x_sem.at[k]) for k, r in enumerate((a0, b0, a1, b1))]
-    for copy in own_x:
-        copy.start()
+    own_x = pltpu.make_async_copy(x_ref, xs.at[OWN], x_sem)
+    own_x.start()
     pl.semaphore_wait(barrier, 2)
 
     heads = [
-        send(x_ref.at[a0], xs.at[FIRST, a0], ag_send.at[0], ag_recv.at[0], right),
-        send(x_ref.at[b0], xs.at[FIRST, b0], ag_send.at[1], ag_recv.at[1], left),
-        send(xs.at[OWN, a1], xs.at[FIRST, a1], ag_send.at[2], ag_recv.at[2], right),
-        send(xs.at[OWN, b1], xs.at[FIRST, b1], ag_send.at[3], ag_recv.at[3], left),
+        send(x_ref.at[a], xs.at[FIRST, a], ag_send.at[0], ag_recv.at[0], right),
+        send(x_ref.at[b], xs.at[FIRST, b], ag_send.at[1], ag_recv.at[1], left),
     ]
     tails = [
-        send(xs.at[OWN, b], xs.at[SECOND, a], ag_send.at[4], ag_recv.at[4], right),
-        send(xs.at[OWN, a], xs.at[SECOND, b], ag_send.at[5], ag_recv.at[5], left),
+        send(xs.at[OWN, b], xs.at[SECOND, a], ag_send.at[2], ag_recv.at[2], right),
+        send(xs.at[OWN, a], xs.at[SECOND, b], ag_send.at[3], ag_recv.at[3], left),
     ]
     onward = [
-        send(xs.at[FIRST, a], xs.at[FAR, a], ag_send.at[6], ag_recv.at[6], right),
-        send(xs.at[FIRST, b], xs.at[FAR, b], ag_send.at[7], ag_recv.at[7], left),
+        send(xs.at[FIRST, a], xs.at[FAR, a], ag_send.at[4], ag_recv.at[4], right),
+        send(xs.at[FIRST, b], xs.at[FAR, b], ag_send.at[5], ag_recv.at[5], left),
     ]
     direct = [
         send(to_dir.at[:, b], by_dir.at[:, b], dir_send.at[0], dir_recv.at[0], right),
@@ -96,12 +90,9 @@
             send(to_mrg.at[j, a], by_mrg.at[j, b], mrg_send.at[j, 1], mrg_recv.at[j, 1], left),
         )
 
-    for copy in heads[:2]:
-        copy.start()
-    for copy in own_x:
-        copy.wait()
-    for copy in heads[2:]:
-        copy.start()
+    for copy in heads:
+        copy.start()
+    own_x.wait()
     for copy in tails:
         copy.start()
 
@@ -214,14 +205,16 @@
 
 def finish(y_ref, own, by_mrg, out_ref, piece, sem):
     last = own.shape[0] - 1
-    done = pl.ds(0, last * TILE_D)
-    rest = pltpu.make_async_copy(y_ref.at[:, done], out_ref.at[:, done], sem.at[0])
-    rest.start()
-    piece[...] = (own[last] + by_mrg[last].astype(F32)).astype(BF16)
-    end = pltpu.make_async_copy(piece, out_ref.at[:, pl.ds(last * TILE_D, TILE_D)], sem.at[1])
-    end.start()
-    rest.wait()
-    end.wait()
+    copies = []
+    for j in range(last + 1):
+        col = pl.ds(j * TILE_D, TILE_D)
+        if j == last:
+            piece[...] = (own[j] + by_mrg[j].astype(F32)).astype(BF16)
+        source = piece if j == last else y_ref.at[:, col]
+        copies.append(pltpu.make_async_copy(source, out_ref.at[:, col], sem.at[j]))
+        copies[-1].start()
+    for copy in copies:
+        copy.wait()
 
 
 def solution(mesh):
@@ -251,8 +244,8 @@
                 pltpu.VMEM(pieces, BF16),
                 pltpu.VMEM(pieces, BF16),
                 pltpu.VMEM(pieces, BF16),
-                dma((4,)), dma((SLOTS_H,)), dma((SLOTS_H,)), dma((SLOTS_D,)),
-                dma((8,)), dma((8,)), dma((2,)), dma((2,)),
+                dma, dma((SLOTS_H,)), dma((SLOTS_H,)), dma((SLOTS_D,)),
+                dma((6,)), dma((6,)), dma((2,)), dma((2,)),
                 dma((n_d, 2)), dma((n_d, 2)), dma((n_d, 2)), dma((n_d, 2)),
             ],
             compiler_params=pltpu.CompilerParams(
@@ -268,7 +261,7 @@
             out_shape=jax.ShapeDtypeStruct((rows, d), BF16),
             in_specs=[vmem] * 3,
             out_specs=pl.BlockSpec(memory_space=pl.ANY),
-            scratch_shapes=[pltpu.VMEM((rows, TILE_D), BF16), dma((2,))],
+            scratch_shapes=[pltpu.VMEM((rows, TILE_D), BF16), dma((n_d,))],
             compiler_params=pltpu.CompilerParams(vmem_limit_bytes=FINISH_MIB * 1024 * 1024),
             name="finish",
         )(*parts)

time: 142 us -> 142 us (level)
  no operation moved by 1% of the time
where the time goes in v7:
time: 142 us
  Pallas kernels  142 us (100%)
    pallas_call x1, Pallas kernels, step(): pl.pallas_call(functools.partial(kernel, n), out_shape=(pltpu.VMEM((rows,...  141 us

profile of v7, /device:TPU:112, one launch (start us, length us, event | category | flops | bytes accessed | tf_op | source)
XLA Modules:
  0.0 142.1 jit_solution(8903927742321519351)
XLA Ops:
  0.0 140.7 %mlp_ring.1 = (bf16[256,4096]{1,0:T(8,128)(2,1)S(1)}, f32[8,256,512]{2,1,0:T(8,128)S(1)}, bf16[8,256,512]{2,1,0:T(8,128)(2,1)S(1)}) custom-call(bf16[256,4096]{1,0:T(8,128)(2,1)} %x_ref.1, bf16[4096,2560]{1,0:T(8,128)(2,1)} %wg_ref.1, bf16[4096,2560]{1,0:T(8,128)(2,1)} %wu_ref.1, bf16[2560,4096]{1,0:T(8,128)(2,1)} %wd_ref.1), custom_call_target="tpu_custom_call" | custom-call | flops 64424509440 | bytes 251658240 | tf_op jit(solution)/shard_map/mlp_ring/pallas_call | solution.py:230
  140.7 1.4 finish.1

commit v8 on v7

--- a/solution.py
+++ b/solution.py
@@ -13,6 +13,7 @@
 
 TILE_H = 256
 TILE_D = 512
+PIECE = 2
 SLOTS_H = 3
 SLOTS_D = 3
 VMEM_MIB = 46
@@ -33,6 +34,7 @@
     half = rows // 2
     n_h = wg_ref.shape[1] // TILE_H
     n_d = d // TILE_D
+    n_p = n_d // PIECE
     passes = xs.shape[0]
     a, b = pl.ds(0, half), pl.ds(half, half)
 
@@ -78,16 +80,21 @@
         send(to_dir.at[:, a], by_dir.at[:, a], dir_send.at[1], dir_recv.at[1], left),
     ]
 
-    def far(j):
+    def tiles(p):
+        return pl.ds(p * PIECE, PIECE)
+
+    def far(p):
+        t = tiles(p)
         return (
-            send(to_far.at[j, a], by_far.at[j, b], far_send.at[j, 0], far_recv.at[j, 0], right),
-            send(to_far.at[j, b], by_far.at[j, a], far_send.at[j, 1], far_recv.at[j, 1], left),
+            send(to_far.at[t, a], by_far.at[t, b], far_send.at[p, 0], far_recv.at[p, 0], right),
+            send(to_far.at[t, b], by_far.at[t, a], far_send.at[p, 1], far_recv.at[p, 1], left),
         )
 
-    def merged(j):
+    def merged(p):
+        t = tiles(p)
         return (
-            send(to_mrg.at[j, b], by_mrg.at[j, a], mrg_send.at[j, 0], mrg_recv.at[j, 0], right),
-            send(to_mrg.at[j, a], by_mrg.at[j, b], mrg_send.at[j, 1], mrg_recv.at[j, 1], left),
+            send(to_mrg.at[t, b], by_mrg.at[t, a], mrg_send.at[p, 0], mrg_recv.at[p, 0], right),
+            send(to_mrg.at[t, a], by_mrg.at[t, b], mrg_send.at[p, 1], mrg_recv.at[p, 1], left),
         )
 
     for copy in heads:
@@ -142,8 +149,11 @@
 
     def put_far(j, term):
         to_far[j] = term.astype(BF16)
-        for copy in far(j):
-            copy.start()
+
+        @pl.when(lax.rem(j, PIECE) == PIECE - 1)
+        def _():
+            for copy in far(lax.div(j, PIECE)):
+                copy.start()
 
     hidden(OWN)
     down(OWN, put_own)
@@ -167,12 +177,17 @@
     hidden(FAR)
     down(FAR, put_far)
 
-    @pl.loop(0, n_d)
-    def _(j):
-        for copy in far(j):
+    @pl.loop(0, n_p)
+    def _(p):
+        for copy in far(p):
             copy.wait_recv()
-        to_mrg[j] = (mid[j] + by_far[j].astype(F32)).astype(BF16)
-        for copy in merged(j):
+
+        @pl.loop(0, PIECE)
+        def _(k):
+            j = p * PIECE + k
+            to_mrg[j] = (mid[j] + by_far[j].astype(F32)).astype(BF16)
+
+        for copy in merged(p):
             copy.start()
 
     for copy in direct:
@@ -180,21 +195,29 @@
     for copy in heads + tails + onward + direct:
         copy.wait_send()
 
-    @pl.loop(0, n_d)
+    @pl.loop(0, n_p)
+    def _(p):
+        for copy in far(p):
+            copy.wait_send()
+
+    last = n_p - 1
+
+    @pl.loop(last * PIECE, n_d)
     def _(j):
-        for copy in far(j):
-            copy.wait_send()
-
-    last = n_d - 1
-    own[last] += by_dir[last].astype(F32)
+        own[j] += by_dir[j].astype(F32)
 
     @pl.loop(0, last)
-    def _(j):
-        for copy in merged(j):
+    def _(p):
+        for copy in merged(p):
             copy.wait_recv()
-        col = pl.ds(pl.multiple_of(j * TILE_D, TILE_D), TILE_D)
-        y_ref[:, col] = (own[j] + by_dir[j].astype(F32) + by_mrg[j].astype(F32)).astype(BF16)
-        for copy in merged(j):
+
+        @pl.loop(0, PIECE)
+        def _(k):
+            j = p * PIECE + k
+            col = pl.ds(pl.multiple_of(j * TILE_D, TILE_D), TILE_D)
+            y_ref[:, col] = (own[j] + by_dir[j].astype(F32) + by_mrg[j].astype(F32)).astype(BF16)
+
+        for copy in merged(p):
             copy.wait_send()
 
     for copy in merged(last):
@@ -204,14 +227,15 @@
 
 
 def finish(y_ref, own, by_mrg, out_ref, piece, sem):
-    last = own.shape[0] - 1
-    copies = []
-    for j in range(last + 1):
-        col = pl.ds(j * TILE_D, TILE_D)
-        if j == last:
-            piece[...] = (own[j] + by_mrg[j].astype(F32)).astype(BF16)
-        source = piece if j == last else y_ref.at[:, col]
-        copies.append(pltpu.make_async_copy(source, out_ref.at[:, col], sem.at[j]))
+    n_d = own.shape[0]
+    done = n_d - PIECE
+    col = pl.ds(0, done * TILE_D)
+    copies = [pltpu.make_async_copy(y_ref.at[:, col], out_ref.at[:, col], sem.at[PIECE])]
+    copies[0].start()
+    for k in range(PIECE):
+        j = done + k
+        piece[k] = (own[j] + by_mrg[j].astype(F32)).astype(BF16)
+        copies.append(pltpu.make_async_copy(piece.at[k], out_ref.at[:, pl.ds(j * TILE_D, TILE_D)], sem.at[k]))
         copies[-1].start()
     for copy in copies:
         copy.wait()
@@ -224,6 +248,7 @@
         rows, d = x.shape
         ff = w_gate.shape[1]
         n_d = d // TILE_D
+        n_p = n_d // PIECE
         dma = pltpu.SemaphoreType.DMA
         pieces = (n_d, rows, TILE_D)
         vmem = pl.BlockSpec(memory_space=pltpu.VMEM)
@@ -246,7 +271,7 @@
                 pltpu.VMEM(pieces, BF16),
                 dma, dma((SLOTS_H,)), dma((SLOTS_H,)), dma((SLOTS_D,)),
                 dma((6,)), dma((6,)), dma((2,)), dma((2,)),
-                dma((n_d, 2)), dma((n_d, 2)), dma((n_d, 2)), dma((n_d, 2)),
+                dma((n_p, 2)), dma((n_p, 2)), dma((n_p, 2)), dma((n_p, 2)),
             ],
             compiler_params=pltpu.CompilerParams(
                 collective_id=0, has_side_effects=True, vmem_limit_bytes=VMEM_MIB * 1024 * 1024
@@ -261,7 +286,7 @@
             out_shape=jax.ShapeDtypeStruct((rows, d), BF16),
             in_specs=[vmem] * 3,
             out_specs=pl.BlockSpec(memory_space=pl.ANY),
-            scratch_shapes=[pltpu.VMEM((rows, TILE_D), BF16), dma((n_d,))],
+            scratch_shapes=[pltpu.VMEM((PIECE, rows, TILE_D), BF16), dma((PIECE + 1,))],
             compiler_params=pltpu.CompilerParams(vmem_limit_bytes=FINISH_MIB * 1024 * 1024),
             name="finish",
         )(*parts)

time: 142 us -> 142 us (level)
  no operation moved by 1% of the time
where the time goes in v8:
time: 142 us
  Pallas kernels  142 us (100%)
    pallas_call x1, Pallas kernels, step(): pl.pallas_call(functools.partial(kernel, n), out_shape=(pltpu.VMEM((rows,...  140 us

profile of v8, /device:TPU:112, one launch (start us, length us, event | category | flops | bytes accessed | tf_op | source)
XLA Modules:
  0.0 141.7 jit_solution(10627795208369464306)
XLA Ops:
  0.0 140.4 %mlp_ring.1 = (bf16[256,4096]{1,0:T(8,128)(2,1)S(1)}, f32[8,256,512]{2,1,0:T(8,128)S(1)}, bf16[8,256,512]{2,1,0:T(8,128)(2,1)S(1)}) custom-call(bf16[256,4096]{1,0:T(8,128)(2,1)} %x_ref.1, bf16[4096,2560]{1,0:T(8,128)(2,1)} %wg_ref.1, bf16[4096,2560]{1,0:T(8,128)(2,1)} %wu_ref.1, bf16[2560,4096]{1,0:T(8,128)(2,1)} %wd_ref.1), custom_call_target="tpu_custom_call" | custom-call | flops 64424509440 | bytes 251658240 | tf_op jit(solution)/shard_map/mlp_ring/pallas_call | solution.py:255
  140.4 1.3 finish.1

commit v9 on v8

--- a/solution.py
+++ b/solution.py
@@ -13,7 +13,7 @@
 
 TILE_H = 256
 TILE_D = 512
-PIECE = 2
+PIECE = 4
 SLOTS_H = 3
 SLOTS_D = 3
 VMEM_MIB = 46

time: 142 us -> 142 us (level)
  no operation moved by 1% of the time
where the time goes in v9:
time: 142 us
  Pallas kernels  142 us (100%)
    pallas_call x1, Pallas kernels, step(): pl.pallas_call(functools.partial(kernel, n), out_shape=(pltpu.VMEM((rows,...  140 us

profile of v9, /device:TPU:112, one launch (start us, length us, event | category | flops | bytes accessed | tf_op | source)
XLA Modules:
  0.0 141.6 jit_solution(7405294466221443147)
XLA Ops:
  0.0 140.2 %mlp_ring.1 = (bf16[256,4096]{1,0:T(8,128)(2,1)S(1)}, f32[8,256,512]{2,1,0:T(8,128)S(1)}, bf16[8,256,512]{2,1,0:T(8,128)(2,1)S(1)}) custom-call(bf16[256,4096]{1,0:T(8,128)(2,1)} %x_ref.1, bf16[4096,2560]{1,0:T(8,128)(2,1)} %wg_ref.1, bf16[4096,2560]{1,0:T(8,128)(2,1)} %wu_ref.1, bf16[2560,4096]{1,0:T(8,128)(2,1)} %wd_ref.1), custom_call_target="tpu_custom_call" | custom-call | flops 64424509440 | bytes 251658240 | tf_op jit(solution)/shard_map/mlp_ring/pallas_call | solution.py:255
  140.3 1.4 finish.1

commit v10 on v9

--- a/solution.py
+++ b/solution.py
@@ -13,10 +13,10 @@
 
 TILE_H = 256
 TILE_D = 512
-PIECE = 4
+BACK = 2
 SLOTS_H = 3
 SLOTS_D = 3
-VMEM_MIB = 46
+VMEM_MIB = 48
 FINISH_MIB = 4
 
 OWN, FIRST, SECOND, FAR = range(4)
@@ -34,7 +34,7 @@
     half = rows // 2
     n_h = wg_ref.shape[1] // TILE_H
     n_d = d // TILE_D
-    n_p = n_d // PIECE
+    pieces = ((0, n_d - BACK), (n_d - BACK, n_d))
     passes = xs.shape[0]
     a, b = pl.ds(0, half), pl.ds(half, half)
 
@@ -80,18 +80,15 @@
         send(to_dir.at[:, a], by_dir.at[:, a], dir_send.at[1], dir_recv.at[1], left),
     ]
 
-    def tiles(p):
-        return pl.ds(p * PIECE, PIECE)
-
     def far(p):
-        t = tiles(p)
+        t = pl.ds(pieces[p][0], pieces[p][1] - pieces[p][0])
         return (
             send(to_far.at[t, a], by_far.at[t, b], far_send.at[p, 0], far_recv.at[p, 0], right),
             send(to_far.at[t, b], by_far.at[t, a], far_send.at[p, 1], far_recv.at[p, 1], left),
         )
 
     def merged(p):
-        t = tiles(p)
+        t = pl.ds(pieces[p][0], pieces[p][1] - pieces[p][0])
         return (
             send(to_mrg.at[t, b], by_mrg.at[t, a], mrg_send.at[p, 0], mrg_recv.at[p, 0], right),
             send(to_mrg.at[t, a], by_mrg.at[t, b], mrg_send.at[p, 1], mrg_recv.at[p, 1], left),
@@ -119,20 +116,20 @@
             gate = jnp.dot(xs[p], wg[s], preferred_element_type=F32)
             up = jnp.dot(xs[p], wu[s], preferred_element_type=F32)
             col = pl.ds(pl.multiple_of(i * TILE_H, TILE_H), TILE_H)
-            hid[:, col] = (jax.nn.gelu(gate) * up).astype(BF16)
+            hid[min(p, 1), :, col] = (jax.nn.gelu(gate) * up).astype(BF16)
 
             @pl.when(g + SLOTS_H < passes * n_h)
             def _():
                 for copy in load_h(g + SLOTS_H):
                     copy.start()
 
-    def down(p, put):
+    def down(turn, p, put):
         @pl.loop(0, n_d)
         def _(j):
-            g = p * n_d + j
+            g = turn * n_d + j
             s = lax.rem(g, SLOTS_D)
             load_d(g).wait()
-            put(j, jnp.dot(hid[...], wd[s], preferred_element_type=F32))
+            put(j, jnp.dot(hid[min(p, 1)], wd[s], preferred_element_type=F32))
 
             @pl.when(g + SLOTS_D < passes * n_d)
             def _():
@@ -150,41 +147,41 @@
     def put_far(j, term):
         to_far[j] = term.astype(BF16)
 
-        @pl.when(lax.rem(j, PIECE) == PIECE - 1)
-        def _():
-            for copy in far(lax.div(j, PIECE)):
-                copy.start()
+        for p, (_, end) in enumerate(pieces):
+
+            @pl.when(j == end - 1)
+            def _():
+                for copy in far(p):
+                    copy.start()
 
     hidden(OWN)
-    down(OWN, put_own)
 
     for copy in heads:
         copy.wait_recv()
     for copy in onward:
         copy.start()
     hidden(FIRST)
-    down(FIRST, put_direct)
+    down(0, FIRST, put_direct)
     for copy in direct:
         copy.start()
 
     for copy in tails:
         copy.wait_recv()
     hidden(SECOND)
-    down(SECOND, put_mid)
+    down(1, SECOND, put_mid)
 
     for copy in onward:
         copy.wait_recv()
     hidden(FAR)
-    down(FAR, put_far)
-
-    @pl.loop(0, n_p)
-    def _(p):
+    down(2, FAR, put_far)
+    down(3, OWN, put_own)
+
+    for p, (start, end) in enumerate(pieces):
         for copy in far(p):
             copy.wait_recv()
 
-        @pl.loop(0, PIECE)
-        def _(k):
-            j = p * PIECE + k
+        @pl.loop(start, end)
+        def _(j):
             to_mrg[j] = (mid[j] + by_far[j].astype(F32)).astype(BF16)
 
         for copy in merged(p):
@@ -192,47 +189,35 @@
 
     for copy in direct:
         copy.wait_recv()
-    for copy in heads + tails + onward + direct:
-        copy.wait_send()
-
-    @pl.loop(0, n_p)
-    def _(p):
-        for copy in far(p):
-            copy.wait_send()
-
-    last = n_p - 1
-
-    @pl.loop(last * PIECE, n_d)
+
+    @pl.loop(0, n_d)
     def _(j):
         own[j] += by_dir[j].astype(F32)
 
-    @pl.loop(0, last)
-    def _(p):
-        for copy in merged(p):
-            copy.wait_recv()
-
-        @pl.loop(0, PIECE)
-        def _(k):
-            j = p * PIECE + k
-            col = pl.ds(pl.multiple_of(j * TILE_D, TILE_D), TILE_D)
-            y_ref[:, col] = (own[j] + by_dir[j].astype(F32) + by_mrg[j].astype(F32)).astype(BF16)
-
-        for copy in merged(p):
-            copy.wait_send()
-
-    for copy in merged(last):
-        copy.wait_recv()
-    for copy in merged(last):
+    for copy in heads + tails + onward + [*direct, *far(0), *far(1)]:
         copy.wait_send()
+    for copy in merged(0):
+        copy.wait_recv()
+
+    @pl.loop(*pieces[0])
+    def _(j):
+        col = pl.ds(pl.multiple_of(j * TILE_D, TILE_D), TILE_D)
+        y_ref[:, col] = (own[j] + by_mrg[j].astype(F32)).astype(BF16)
+
+    for copy in merged(0):
+        copy.wait_send()
+    for copy in merged(1):
+        copy.wait_recv()
+    for copy in merged(1):
+        copy.wait_send()
 
 
 def finish(y_ref, own, by_mrg, out_ref, piece, sem):
-    n_d = own.shape[0]
-    done = n_d - PIECE
+    done = own.shape[0] - BACK
     col = pl.ds(0, done * TILE_D)
-    copies = [pltpu.make_async_copy(y_ref.at[:, col], out_ref.at[:, col], sem.at[PIECE])]
+    copies = [pltpu.make_async_copy(y_ref.at[:, col], out_ref.at[:, col], sem.at[BACK])]
     copies[0].start()
-    for k in range(PIECE):
+    for k in range(BACK):
         j = done + k
         piece[k] = (own[j] + by_mrg[j].astype(F32)).astype(BF16)
         copies.append(pltpu.make_async_copy(piece.at[k], out_ref.at[:, pl.ds(j * TILE_D, TILE_D)], sem.at[k]))
@@ -248,7 +233,6 @@
         rows, d = x.shape
         ff = w_gate.shape[1]
         n_d = d // TILE_D
-        n_p = n_d // PIECE
         dma = pltpu.SemaphoreType.DMA
         pieces = (n_d, rows, TILE_D)
         vmem = pl.BlockSpec(memory_space=pltpu.VMEM)
@@ -259,7 +243,7 @@
             out_specs=(vmem, vmem, vmem),
             scratch_shapes=[
                 pltpu.VMEM((n, rows, d), BF16),
-                pltpu.VMEM((rows, ff), BF16),
+                pltpu.VMEM((2, rows, ff), BF16),
                 pltpu.VMEM((SLOTS_H, d, TILE_H), BF16),
                 pltpu.VMEM((SLOTS_H, d, TILE_H), BF16),
                 pltpu.VMEM((SLOTS_D, ff, TILE_D), BF16),
@@ -271,7 +255,7 @@
                 pltpu.VMEM(pieces, BF16),
                 dma, dma((SLOTS_H,)), dma((SLOTS_H,)), dma((SLOTS_D,)),
                 dma((6,)), dma((6,)), dma((2,)), dma((2,)),
-                dma((n_p, 2)), dma((n_p, 2)), dma((n_p, 2)), dma((n_p, 2)),
+                dma((2, 2)), dma((2, 2)), dma((2, 2)), dma((2, 2)),
             ],
             compiler_params=pltpu.CompilerParams(
                 collective_id=0, has_side_effects=True, vmem_limit_bytes=VMEM_MIB * 1024 * 1024
@@ -286,7 +270,7 @@
             out_shape=jax.ShapeDtypeStruct((rows, d), BF16),
             in_specs=[vmem] * 3,
             out_specs=pl.BlockSpec(memory_space=pl.ANY),
-            scratch_shapes=[pltpu.VMEM((PIECE, rows, TILE_D), BF16), dma((PIECE + 1,))],
+            scratch_shapes=[pltpu.VMEM((BACK, rows, TILE_D), BF16), dma((BACK + 1,))],
             compiler_params=pltpu.CompilerParams(vmem_limit_bytes=FINISH_MIB * 1024 * 1024),
             name="finish",
         )(*parts)

time: 142 us -> 142 us (level)
  no operation moved by 1% of the time
where the time goes in v10:
time: 142 us
  Pallas kernels  142 us (100%)
    pallas_call x1, Pallas kernels, step(): pl.pallas_call(functools.partial(kernel, n), out_shape=(pltpu.VMEM((rows,...  140 us

profile of v10, /device:TPU:112, one launch (start us, length us, event | category | flops | bytes accessed | tf_op | source)
XLA Modules:
  0.0 141.6 jit_solution(10827883969091872484)
XLA Ops:
  0.0 140.2 %mlp_ring.1 = (bf16[256,4096]{1,0:T(8,128)(2,1)S(1)}, f32[8,256,512]{2,1,0:T(8,128)S(1)}, bf16[8,256,512]{2,1,0:T(8,128)(2,1)S(1)}) custom-call(bf16[256,4096]{1,0:T(8,128)(2,1)} %x_ref.1, bf16[4096,2560]{1,0:T(8,128)(2,1)} %wg_ref.1, bf16[4096,2560]{1,0:T(8,128)(2,1)} %wu_ref.1, bf16[2560,4096]{1,0:T(8,128)(2,1)} %wd_ref.1), custom_call_target="tpu_custom_call" | custom-call | flops 64424509440 | bytes 251658240 | tf_op jit(solution)/shard_map/mlp_ring/pallas_call | solution.py:239
  140.3 1.3 finish.1

commit v11 on v10

--- a/solution.py
+++ b/solution.py
@@ -59,13 +59,14 @@
     barrier = pltpu.get_barrier_semaphore()
     for neighbour in (left, right):
         pl.semaphore_signal(barrier, inc=1, device_id={"tp": neighbour}, device_id_type=MESH)
-    own_x = pltpu.make_async_copy(x_ref, xs.at[OWN], x_sem)
-    own_x.start()
+    own_x = [pltpu.make_async_copy(x_ref.at[h], xs.at[OWN, h], x_sem.at[k]) for k, h in enumerate((b, a))]
+    for copy in own_x:
+        copy.start()
     pl.semaphore_wait(barrier, 2)
 
     heads = [
         send(x_ref.at[a], xs.at[FIRST, a], ag_send.at[0], ag_recv.at[0], right),
-        send(x_ref.at[b], xs.at[FIRST, b], ag_send.at[1], ag_recv.at[1], left),
+        send(xs.at[OWN, b], xs.at[FIRST, b], ag_send.at[1], ag_recv.at[1], left),
     ]
     tails = [
         send(xs.at[OWN, b], xs.at[SECOND, a], ag_send.at[2], ag_recv.at[2], right),
@@ -94,9 +95,10 @@
             send(to_mrg.at[t, a], by_mrg.at[t, b], mrg_send.at[p, 1], mrg_recv.at[p, 1], left),
         )
 
-    for copy in heads:
-        copy.start()
-    own_x.wait()
+    heads[0].start()
+    own_x[0].wait()
+    heads[1].start()
+    own_x[1].wait()
     for copy in tails:
         copy.start()
 
@@ -253,7 +255,7 @@
                 pltpu.VMEM(pieces, BF16),
                 pltpu.VMEM(pieces, BF16),
                 pltpu.VMEM(pieces, BF16),
-                dma, dma((SLOTS_H,)), dma((SLOTS_H,)), dma((SLOTS_D,)),
+                dma((2,)), dma((SLOTS_H,)), dma((SLOTS_H,)), dma((SLOTS_D,)),
                 dma((6,)), dma((6,)), dma((2,)), dma((2,)),
                 dma((2, 2)), dma((2, 2)), dma((2, 2)), dma((2, 2)),
             ],

time: 142 us -> 142 us (level)
  no operation moved by 1% of the time
where the time goes in v11:
time: 142 us
  Pallas kernels  142 us (100%)
    pallas_call x1, Pallas kernels, step(): pl.pallas_call(functools.partial(kernel, n), out_shape=(pltpu.VMEM((rows,...  140 us

profile of v11, /device:TPU:112, one launch (start us, length us, event | category | flops | bytes accessed | tf_op | source)
XLA Modules:
  0.0 141.6 jit_solution(8153989300535048661)
XLA Ops:
  0.0 140.3 %mlp_ring.1 = (bf16[256,4096]{1,0:T(8,128)(2,1)S(1)}, f32[8,256,512]{2,1,0:T(8,128)S(1)}, bf16[8,256,512]{2,1,0:T(8,128)(2,1)S(1)}) custom-call(bf16[256,4096]{1,0:T(8,128)(2,1)} %x_ref.1, bf16[4096,2560]{1,0:T(8,128)(2,1)} %wg_ref.1, bf16[4096,2560]{1,0:T(8,128)(2,1)} %wu_ref.1, bf16[2560,4096]{1,0:T(8,128)(2,1)} %wd_ref.1), custom_call_target="tpu_custom_call" | custom-call | flops 64424509440 | bytes 251658240 | tf_op jit(solution)/shard_map/mlp_ring/pallas_call | solution.py:241
  140.3 1.3 finish.1

commit v12 on v10

--- a/solution.py
+++ b/solution.py
@@ -59,8 +59,6 @@
     barrier = pltpu.get_barrier_semaphore()
     for neighbour in (left, right):
         pl.semaphore_signal(barrier, inc=1, device_id={"tp": neighbour}, device_id_type=MESH)
-    own_x = pltpu.make_async_copy(x_ref, xs.at[OWN], x_sem)
-    own_x.start()
     pl.semaphore_wait(barrier, 2)
 
     heads = [
@@ -96,6 +94,8 @@
 
     for copy in heads:
         copy.start()
+    own_x = pltpu.make_async_copy(x_ref, xs.at[OWN], x_sem)
+    own_x.start()
     own_x.wait()
     for copy in tails:
         copy.start()
@@ -212,16 +212,19 @@
         copy.wait_send()
 
 
-def finish(y_ref, own, by_mrg, out_ref, piece, sem):
-    done = own.shape[0] - BACK
-    col = pl.ds(0, done * TILE_D)
-    copies = [pltpu.make_async_copy(y_ref.at[:, col], out_ref.at[:, col], sem.at[BACK])]
+def finish(y_ref, own, by_mrg, out_ref, back, sem):
+    n_d = own.shape[0]
+    done = (n_d - BACK) * TILE_D
+    first, second = pl.ds(0, done), pl.ds(done, BACK * TILE_D)
+    copies = [
+        pltpu.make_async_copy(y_ref.at[:, first], out_ref.at[:, first], sem.at[0]),
+        pltpu.make_async_copy(back, out_ref.at[:, second], sem.at[1]),
+    ]
     copies[0].start()
     for k in range(BACK):
-        j = done + k
-        piece[k] = (own[j] + by_mrg[j].astype(F32)).astype(BF16)
-        copies.append(pltpu.make_async_copy(piece.at[k], out_ref.at[:, pl.ds(j * TILE_D, TILE_D)], sem.at[k]))
-        copies[-1].start()
+        j = n_d - BACK + k
+        back[:, pl.ds(k * TILE_D, TILE_D)] = (own[j] + by_mrg[j].astype(F32)).astype(BF16)
+    copies[1].start()
     for copy in copies:
         copy.wait()
 
@@ -270,7 +273,7 @@
             out_shape=jax.ShapeDtypeStruct((rows, d), BF16),
             in_specs=[vmem] * 3,
             out_specs=pl.BlockSpec(memory_space=pl.ANY),
-            scratch_shapes=[pltpu.VMEM((BACK, rows, TILE_D), BF16), dma((BACK + 1,))],
+            scratch_shapes=[pltpu.VMEM((rows, BACK * TILE_D), BF16), dma((2,))],
             compiler_params=pltpu.CompilerParams(vmem_limit_bytes=FINISH_MIB * 1024 * 1024),
             name="finish",
         )(*parts)

time: 142 us -> 142 us (level)
  no operation moved by 1% of the time
where the time goes in v12:
time: 142 us
  Pallas kernels  142 us (100%)
    pallas_call x1, Pallas kernels, step(): pl.pallas_call(functools.partial(kernel, n), out_shape=(pltpu.VMEM((rows,...  140 us

profile of v12, /device:TPU:112, one launch (start us, length us, event | category | flops | bytes accessed | tf_op | source)
XLA Modules:
  0.0 141.6 jit_solution(14965441838083528244)
XLA Ops:
  0.0 140.2 %mlp_ring.1 = (bf16[256,4096]{1,0:T(8,128)(2,1)S(1)}, f32[8,256,512]{2,1,0:T(8,128)S(1)}, bf16[8,256,512]{2,1,0:T(8,128)(2,1)S(1)}) custom-call(bf16[256,4096]{1,0:T(8,128)(2,1)} %x_ref.1, bf16[4096,2560]{1,0:T(8,128)(2,1)} %wg_ref.1, bf16[4096,2560]{1,0:T(8,128)(2,1)} %wu_ref.1, bf16[2560,4096]{1,0:T(8,128)(2,1)} %wd_ref.1), custom_call_target="tpu_custom_call" | custom-call | flops 64424509440 | bytes 251658240 | tf_op jit(solution)/shard_map/mlp_ring/pallas_call | solution.py:242
  140.3 1.3 finish.1

commit v13 on v10

--- a/solution.py
+++ b/solution.py
@@ -76,22 +76,22 @@
         send(xs.at[FIRST, b], xs.at[FAR, b], ag_send.at[5], ag_recv.at[5], left),
     ]
     direct = [
-        send(to_dir.at[:, b], by_dir.at[:, b], dir_send.at[0], dir_recv.at[0], right),
-        send(to_dir.at[:, a], by_dir.at[:, a], dir_send.at[1], dir_recv.at[1], left),
+        send(to_dir.at[1], by_dir.at[1], dir_send.at[0], dir_recv.at[0], right),
+        send(to_dir.at[0], by_dir.at[0], dir_send.at[1], dir_recv.at[1], left),
     ]
 
     def far(p):
         t = pl.ds(pieces[p][0], pieces[p][1] - pieces[p][0])
         return (
-            send(to_far.at[t, a], by_far.at[t, b], far_send.at[p, 0], far_recv.at[p, 0], right),
-            send(to_far.at[t, b], by_far.at[t, a], far_send.at[p, 1], far_recv.at[p, 1], left),
+            send(to_far.at[0, t], by_far.at[1, t], far_send.at[p, 0], far_recv.at[p, 0], right),
+            send(to_far.at[1, t], by_far.at[0, t], far_send.at[p, 1], far_recv.at[p, 1], left),
         )
 
     def merged(p):
         t = pl.ds(pieces[p][0], pieces[p][1] - pieces[p][0])
         return (
-            send(to_mrg.at[t, b], by_mrg.at[t, a], mrg_send.at[p, 0], mrg_recv.at[p, 0], right),
-            send(to_mrg.at[t, a], by_mrg.at[t, b], mrg_send.at[p, 1], mrg_recv.at[p, 1], left),
+            send(to_mrg.at[1, t], by_mrg.at[0, t], mrg_send.at[p, 0], mrg_recv.at[p, 0], right),
+            send(to_mrg.at[0, t], by_mrg.at[1, t], mrg_send.at[p, 1], mrg_recv.at[p, 1], left),
         )
 
     for copy in heads:
@@ -139,13 +139,15 @@
         own[j] = term
 
     def put_direct(j, term):
-        to_dir[j] = term.astype(BF16)
+        for k, h in enumerate((a, b)):
+            to_dir[k, j] = term[h.start : h.start + half].astype(BF16)
 
     def put_mid(j, term):
         mid[j] = term
 
     def put_far(j, term):
-        to_far[j] = term.astype(BF16)
+        for k, h in enumerate((a, b)):
+            to_far[k, j] = term[h.start : h.start + half].astype(BF16)
 
         for p, (_, end) in enumerate(pieces):
 
@@ -182,7 +184,8 @@
 
         @pl.loop(start, end)
         def _(j):
-            to_mrg[j] = (mid[j] + by_far[j].astype(F32)).astype(BF16)
+            for k, h in enumerate((a, b)):
+                to_mrg[k, j] = (mid[j, h] + by_far[k, j].astype(F32)).astype(BF16)
 
         for copy in merged(p):
             copy.start()
@@ -192,7 +195,8 @@
 
     @pl.loop(0, n_d)
     def _(j):
-        own[j] += by_dir[j].astype(F32)
+        for k, h in enumerate((a, b)):
+            own[j, h] += by_dir[k, j].astype(F32)
 
     for copy in heads + tails + onward + [*direct, *far(0), *far(1)]:
         copy.wait_send()
@@ -202,7 +206,8 @@
     @pl.loop(*pieces[0])
     def _(j):
         col = pl.ds(pl.multiple_of(j * TILE_D, TILE_D), TILE_D)
-        y_ref[:, col] = (own[j] + by_mrg[j].astype(F32)).astype(BF16)
+        for k, h in enumerate((a, b)):
+            y_ref[h, col] = (own[j, h] + by_mrg[k, j].astype(F32)).astype(BF16)
 
     for copy in merged(0):
         copy.wait_send()
@@ -219,7 +224,10 @@
     copies[0].start()
     for k in range(BACK):
         j = done + k
-        piece[k] = (own[j] + by_mrg[j].astype(F32)).astype(BF16)
+        half = by_mrg.shape[2]
+        for i in range(2):
+            h = pl.ds(i * half, half)
+            piece[k, h] = (own[j, h] + by_mrg[i, j].astype(F32)).astype(BF16)
         copies.append(pltpu.make_async_copy(piece.at[k], out_ref.at[:, pl.ds(j * TILE_D, TILE_D)], sem.at[k]))
         copies[-1].start()
     for copy in copies:
@@ -234,11 +242,12 @@
         ff = w_gate.shape[1]
         n_d = d // TILE_D
         dma = pltpu.SemaphoreType.DMA
-        pieces = (n_d, rows, TILE_D)
+        terms = (n_d, rows, TILE_D)
+        halves = (2, n_d, rows // 2, TILE_D)
         vmem = pl.BlockSpec(memory_space=pltpu.VMEM)
         parts = pl.pallas_call(
             functools.partial(kernel, n),
-            out_shape=(pltpu.VMEM((rows, d), BF16), pltpu.VMEM(pieces, F32), pltpu.VMEM(pieces, BF16)),
+            out_shape=(pltpu.VMEM((rows, d), BF16), pltpu.VMEM(terms, F32), pltpu.VMEM(halves, BF16)),
             in_specs=[pl.BlockSpec(memory_space=pl.ANY)] * 4,
             out_specs=(vmem, vmem, vmem),
             scratch_shapes=[
@@ -247,12 +256,12 @@
                 pltpu.VMEM((SLOTS_H, d, TILE_H), BF16),
                 pltpu.VMEM((SLOTS_H, d, TILE_H), BF16),
                 pltpu.VMEM((SLOTS_D, ff, TILE_D), BF16),
-                pltpu.VMEM(pieces, F32),
-                pltpu.VMEM(pieces, BF16),
-                pltpu.VMEM(pieces, BF16),
-                pltpu.VMEM(pieces, BF16),
-                pltpu.VMEM(pieces, BF16),
-                pltpu.VMEM(pieces, BF16),
+                pltpu.VMEM(terms, F32),
+                pltpu.VMEM(halves, BF16),
+                pltpu.VMEM(halves, BF16),
+                pltpu.VMEM(halves, BF16),
+                pltpu.VMEM(halves, BF16),
+                pltpu.VMEM(halves, BF16),
                 dma, dma((SLOTS_H,)), dma((SLOTS_H,)), dma((SLOTS_D,)),
                 dma((6,)), dma((6,)), dma((2,)), dma((2,)),
                 dma((2, 2)), dma((2, 2)), dma((2, 2)), dma((2, 2)),

time: 142 us -> 142 us (level)
  no operation moved by 1% of the time
where the time goes in v13:
time: 142 us
  Pallas kernels  142 us (100%)
    pallas_call x1, Pallas kernels, step(): pl.pallas_call(functools.partial(kernel, n), out_shape=(pltpu.VMEM((rows,...  140 us

profile of v13, /device:TPU:112, one launch (start us, length us, event | category | flops | bytes accessed | tf_op | source)
XLA Modules:
  0.0 141.6 jit_solution(12110292219990287441)
XLA Ops:
  0.0 140.2 %mlp_ring.1 = (bf16[256,4096]{1,0:T(8,128)(2,1)S(1)}, f32[8,256,512]{2,1,0:T(8,128)S(1)}, bf16[2,8,128,512]{3,2,1,0:T(8,128)(2,1)S(1)}) custom-call(bf16[256,4096]{1,0:T(8,128)(2,1)} %x_ref.1, bf16[4096,2560]{1,0:T(8,128)(2,1)} %wg_ref.1, bf16[4096,2560]{1,0:T(8,128)(2,1)} %wu_ref.1, bf16[2560,4096]{1,0:T(8,128)(2,1)} %wd_ref.1), custom_call_target="tpu_custom_call" | custom-call | flops 64424509440 | bytes 251658240 | tf_op jit(solution)/shard_map/mlp_ring/pallas_call | solution.py:248
  140.3 1.3 finish.1

commit v14 on v13

--- a/solution.py
+++ b/solution.py
@@ -26,7 +26,7 @@
     n,
     x_ref, wg_ref, wu_ref, wd_ref, y_ref, own, by_mrg,
     xs, hid, wg, wu, wd, mid, to_dir, to_far, to_mrg, by_dir, by_far,
-    x_sem, wg_sem, wu_sem, wd_sem, ag_send, ag_recv, dir_send, dir_recv, far_send, far_recv, mrg_send, mrg_recv,
+    ready, x_sem, wg_sem, wu_sem, wd_sem, ag_send, ag_recv, dir_send, dir_recv, far_send, far_recv, mrg_send, mrg_recv,
 ):
     me = lax.axis_index("tp")
     right, left = lax.rem(me + 1, n), lax.rem(me + n - 1, n)
@@ -57,11 +57,10 @@
         )
 
     barrier = pltpu.get_barrier_semaphore()
-    for neighbour in (left, right):
-        pl.semaphore_signal(barrier, inc=1, device_id={"tp": neighbour}, device_id_type=MESH)
+    pl.semaphore_signal(barrier, inc=1, device_id={"tp": left}, device_id_type=MESH)
     own_x = pltpu.make_async_copy(x_ref, xs.at[OWN], x_sem)
     own_x.start()
-    pl.semaphore_wait(barrier, 2)
+    pl.semaphore_wait(barrier, 1)
 
     heads = [
         send(x_ref.at[a], xs.at[FIRST, a], ag_send.at[0], ag_recv.at[0], right),
@@ -94,8 +93,10 @@
             send(to_mrg.at[0, t], by_mrg.at[1, t], mrg_send.at[p, 1], mrg_recv.at[p, 1], left),
         )
 
-    for copy in heads:
-        copy.start()
+    pl.semaphore_signal(ready, inc=1, device_id={"tp": right}, device_id_type=MESH)
+    heads[0].start()
+    pl.semaphore_wait(ready, 1)
+    heads[1].start()
     own_x.wait()
     for copy in tails:
         copy.start()
@@ -262,7 +263,7 @@
                 pltpu.VMEM(halves, BF16),
                 pltpu.VMEM(halves, BF16),
                 pltpu.VMEM(halves, BF16),
-                dma, dma((SLOTS_H,)), dma((SLOTS_H,)), dma((SLOTS_D,)),
+                pltpu.SemaphoreType.REGULAR, dma, dma((SLOTS_H,)), dma((SLOTS_H,)), dma((SLOTS_D,)),
                 dma((6,)), dma((6,)), dma((2,)), dma((2,)),
                 dma((2, 2)), dma((2, 2)), dma((2, 2)), dma((2, 2)),
             ],

time: 142 us -> 141 us (level)
  no operation moved by 1% of the time
where the time goes in v14:
time: 141 us
  Pallas kernels  141 us (100%)
    pallas_call x1, Pallas kernels, step(): pl.pallas_call(functools.partial(kernel, n), out_shape=(pltpu.VMEM((rows,...  140 us

profile of v14, /device:TPU:112, one launch (start us, length us, event | category | flops | bytes accessed | tf_op | source)
XLA Modules:
  0.0 141.2 jit_solution(5087558779552012043)
XLA Ops:
  0.0 139.8 %mlp_ring.1 = (bf16[256,4096]{1,0:T(8,128)(2,1)S(1)}, f32[8,256,512]{2,1,0:T(8,128)S(1)}, bf16[2,8,128,512]{3,2,1,0:T(8,128)(2,1)S(1)}) custom-call(bf16[256,4096]{1,0:T(8,128)(2,1)} %x_ref.1, bf16[4096,2560]{1,0:T(8,128)(2,1)} %wg_ref.1, bf16[4096,2560]{1,0:T(8,128)(2,1)} %wu_ref.1, bf16[2560,4096]{1,0:T(8,128)(2,1)} %wd_ref.1), custom_call_target="tpu_custom_call" | custom-call | flops 64424509440 | bytes 251658240 | tf_op jit(solution)/shard_map/mlp_ring/pallas_call | solution.py:249
  139.9 1.3 finish.1

commit v15 on v14

v15 whole, which is shorter than its diff:
```python
import functools

import jax
import jax.numpy as jnp
from jax import lax
from jax.experimental import pallas as pl
from jax.experimental.pallas import tpu as pltpu
from jax.sharding import PartitionSpec as P

MESH = pl.DeviceIdType.MESH
F32 = jnp.float32
BF16 = jnp.bfloat16

TILE_H = 256
TILE_D = 512
BACK = 2
SLOTS_H = 3
SLOTS_D = 3
VMEM_MIB = 48
FINISH_MIB = 4

OWN, FIRST, SECOND, FAR = range(4)


def kernel(
    n,
    x_ref, wg_ref, wu_ref, wd_ref, y_ref, own, by_mrg,
    xs, hid, wgu, wd, mid, to_dir, to_far, to_mrg, by_dir, by_far,
    ready, h_sem, d_sem, sent, ag_got, dir_got, far_got, mrg_got,
):
    me = lax.axis_index("tp")
    right, left = lax.rem(me + 1, n), lax.rem(me + n - 1, n)
    rows, d = x_ref.shape
    half = rows // 2
    n_h = wg_ref.shape[1] // TILE_H
    n_d = d // TILE_D
    pieces = ((0, n_d - BACK), (n_d - BACK, n_d))
    passes = xs.shape[0]
    a, b = pl.ds(0, half), pl.ds(half, half)

    def load_h(g):
        col = pl.ds(pl.multiple_of(lax.rem(g, n_h) * TILE_H, TILE_H), TILE_H)
        s = lax.rem(g, SLOTS_H)
        for k, w_ref in enumerate((wg_ref, wu_ref)):
            pltpu.make_async_copy(w_ref.at[:, col], wgu.at[s, k], h_sem.at[s]).start()

    def load_d(g):
        col = pl.ds(pl.multiple_of(lax.rem(g, n_d) * TILE_D, TILE_D), TILE_D)
        s = lax.rem(g, SLOTS_D)
        return pltpu.make_async_copy(wd_ref.at[:, col], wd.at[s], d_sem.at[s])

    def wait_all(ref, sem):
        pltpu.make_async_copy(ref, ref, sem).wait()

    def send(src, dst, recv_sem, way):
        return pltpu.make_async_remote_copy(
            src_ref=src,
            dst_ref=dst,
            send_sem=sent.at[way],
            recv_sem=recv_sem,
            device_id={"tp": (right, left)[way]},
            device_id_type=MESH,
        )

    barrier = pltpu.get_barrier_semaphore()
    pl.semaphore_signal(barrier, inc=1, device_id={"tp": left}, device_id_type=MESH)
    own_x = pltpu.make_async_copy(x_ref, xs.at[OWN], d_sem.at[0])
    own_x.start()
    pl.semaphore_wait(barrier, 1)

    heads = [
        send(x_ref.at[a], xs.at[FIRST, a], ag_got.at[0], 0),
        send(x_ref.at[b], xs.at[FIRST, b], ag_got.at[0], 1),
    ]
    tails = [
        send(xs.at[OWN, b], xs.at[SECOND, a], ag_got.at[1], 0),
        send(xs.at[OWN, a], xs.at[SECOND, b], ag_got.at[1], 1),
    ]
    onward = [
        send(xs.at[FIRST, a], xs.at[FAR, a], ag_got.at[2], 0),
        send(xs.at[FIRST, b], xs.at[FAR, b], ag_got.at[2], 1),
    ]
    direct = [
        send(to_dir.at[1], by_dir.at[1], dir_got, 0),
        send(to_dir.at[0], by_dir.at[0], dir_got, 1),
    ]

    def tiles(p):
        return pl.ds(pieces[p][0], pieces[p][1] - pieces[p][0])

    def far(p):
        t = tiles(p)
        return (
            send(to_far.at[0, t], by_far.at[1, t], far_got.at[p], 0),
            send(to_far.at[1, t], by_far.at[0, t], far_got.at[p], 1),
        )

    def merged(p):
        t = tiles(p)
        return (
            send(to_mrg.at[1, t], by_mrg.at[0, t], mrg_got.at[p], 0),
            send(to_mrg.at[0, t], by_mrg.at[1, t], mrg_got.at[p], 1),
        )

    pl.semaphore_signal(ready, inc=1, device_id={"tp": right}, device_id_type=MESH)
    heads[0].start()
    pl.semaphore_wait(ready, 1)
    heads[1].start()
    own_x.wait()
    for copy in tails:
        copy.start()

    for g in range(SLOTS_H):
        load_h(g)
    for g in range(SLOTS_D):
        load_d(g).start()

    def hidden(p):
        @pl.loop(0, n_h)
        def _(i):
            g = p * n_h + i
            s = lax.rem(g, SLOTS_H)
            wait_all(wgu.at[s], h_sem.at[s])
            gate = jnp.dot(xs[p], wgu[s, 0], preferred_element_type=F32)
            up = jnp.dot(xs[p], wgu[s, 1], preferred_element_type=F32)
            col = pl.ds(pl.multiple_of(i * TILE_H, TILE_H), TILE_H)
            hid[min(p, 1), :, col] = (jax.nn.gelu(gate) * up).astype(BF16)

            @pl.when(g + SLOTS_H < passes * n_h)
            def _():
                load_h(g + SLOTS_H)

    def down(turn, p, put):
        @pl.loop(0, n_d)
        def _(j):
            g = turn * n_d + j
            s = lax.rem(g, SLOTS_D)
            load_d(g).wait()
            put(j, jnp.dot(hid[min(p, 1)], wd[s], preferred_element_type=F32))

            @pl.when(g + SLOTS_D < passes * n_d)
            def _():
                load_d(g + SLOTS_D).start()

    def put_own(j, term):
        own[j] = term

    def put_direct(j, term):
        for k, h in enumerate((a, b)):
            to_dir[k, j] = term[h.start : h.start + half].astype(BF16)

    def put_mid(j, term):
        mid[j] = term

    def put_far(j, term):
        for k, h in enumerate((a, b)):
            to_far[k, j] = term[h.start : h.start + half].astype(BF16)

        for p, (_, end) in enumerate(pieces):

            @pl.when(j == end - 1)
            def _():
                for copy in far(p):
                    copy.start()

    hidden(OWN)

    wait_all(xs.at[FIRST], ag_got.at[0])
    for copy in onward:
        copy.start()
    hidden(FIRST)
    down(0, FIRST, put_direct)
    for copy in direct:
        copy.start()

    wait_all(xs.at[SECOND], ag_got.at[1])
    hidden(SECOND)
    down(1, SECOND, put_mid)

    wait_all(xs.at[FAR], ag_got.at[2])
    hidden(FAR)
    down(2, FAR, put_far)
    down(3, OWN, put_own)

    for p, (start, end) in enumerate(pieces):
        wait_all(by_far.at[:, tiles(p)], far_got.at[p])

        @pl.loop(start, end)
        def _(j):
            for k, h in enumerate((a, b)):
                to_mrg[k, j] = (mid[j, h] + by_far[k, j].astype(F32)).astype(BF16)

        for copy in merged(p):
            copy.start()

    wait_all(by_dir, dir_got)

    @pl.loop(0, n_d)
    def _(j):
        for k, h in enumerate((a, b)):
            own[j, h] += by_dir[k, j].astype(F32)

    wait_all(by_mrg.at[:, tiles(0)], mrg_got.at[0])

    @pl.loop(*pieces[0])
    def _(j):
        col = pl.ds(pl.multiple_of(j * TILE_D, TILE_D), TILE_D)
        for k, h in enumerate((a, b)):
            y_ref[h, col] = (own[j, h] + by_mrg[k, j].astype(F32)).astype(BF16)

    wait_all(by_mrg.at[:, tiles(1)], mrg_got.at[1])
    for way in range(2):
        wait_all(xs.at[pl.ds(0, 3)], sent.at[way])


def finish(y_ref, own, by_mrg, out_ref, back, sem):
    n_d, rows, _ = own.shape
    half = rows // 2
    done = (n_d - BACK) * TILE_D
    first, second = pl.ds(0, done), pl.ds(done, BACK * TILE_D)
    pltpu.make_async_copy(y_ref.at[:, first], out_ref.at[:, first], sem).start()
    for k in range(BACK):
        j = n_d - BACK + k
        for i in range(2):
            h = pl.ds(i * half, half)
            back[h, pl.ds(k * TILE_D, TILE_D)] = (own[j, h] + by_mrg[i, j].astype(F32)).astype(BF16)
    pltpu.make_async_copy(back, out_ref.at[:, second], sem).start()
    pltpu.make_async_copy(y_ref, out_ref, sem).wait()


def solution(mesh):
    n = mesh.shape["tp"]

    def step(x, w_gate, w_up, w_down):
        rows, d = x.shape
        ff = w_gate.shape[1]
        n_d = d // TILE_D
        dma = pltpu.SemaphoreType.DMA
        terms = (n_d, rows, TILE_D)
        halves = (2, n_d, rows // 2, TILE_D)
        vmem = pl.BlockSpec(memory_space=pltpu.VMEM)
        parts = pl.pallas_call(
            functools.partial(kernel, n),
            out_shape=(pltpu.VMEM((rows, d), BF16), pltpu.VMEM(terms, F32), pltpu.VMEM(halves, BF16)),
            in_specs=[pl.BlockSpec(memory_space=pl.ANY)] * 4,
            out_specs=(vmem, vmem, vmem),
            scratch_shapes=[
                pltpu.VMEM((n, rows, d), BF16),
                pltpu.VMEM((2, rows, ff), BF16),
                pltpu.VMEM((SLOTS_H, 2, d, TILE_H), BF16),
                pltpu.VMEM((SLOTS_D, ff, TILE_D), BF16),
                pltpu.VMEM(terms, F32),
                pltpu.VMEM(halves, BF16),
                pltpu.VMEM(halves, BF16),
                pltpu.VMEM(halves, BF16),
                pltpu.VMEM(halves, BF16),
                pltpu.VMEM(halves, BF16),
                pltpu.SemaphoreType.REGULAR, dma((SLOTS_H,)), dma((SLOTS_D,)),
                dma((2,)), dma((3,)), dma, dma((2,)), dma((2,)),
            ],
            compiler_params=pltpu.CompilerParams(
                collective_id=0, has_side_effects=True, vmem_limit_bytes=VMEM_MIB * 1024 * 1024
            ),
            cost_estimate=pl.CostEstimate(
                flops=6 * n * rows * d * ff, bytes_accessed=6 * n * d * ff, transcendentals=n * rows * ff
            ),
            name="mlp_ring",
        )(x, w_gate, w_up, w_down)
        return pl.pallas_call(
            finish,
            out_shape=jax.ShapeDtypeStruct((rows, d), BF16),
            in_specs=[vmem] * 3,
            out_specs=pl.BlockSpec(memory_space=pl.ANY),
            scratch_shapes=[pltpu.VMEM((rows, BACK * TILE_D), BF16), dma],
            compiler_params=pltpu.CompilerParams(vmem_limit_bytes=FINISH_MIB * 1024 * 1024),
            name="finish",
        )(*parts)

    return jax.shard_map(
        step,
        mesh=mesh,
        in_specs=(P(("dp", "tp"), None), P(None, "tp"), P(None, "tp"), P("tp", None)),
        out_specs=P(("dp", "tp"), None),
        check_vma=False,
    )
```

time: 141 us -> 141 us (level)
  no operation moved by 1% of the time
where the time goes in v15:
time: 141 us
  Pallas kernels  141 us (100%)
    pallas_call x1, Pallas kernels, step(): pl.pallas_call(functools.partial(kernel, n), out_shape=(pltpu.VMEM((rows,...  140 us

profile of v15, /device:TPU:112, one launch (start us, length us, event | category | flops | bytes accessed | tf_op | source)
XLA Modules:
  0.0 140.9 jit_solution(3846001825189249658)
XLA Ops:
  0.0 139.6 %mlp_ring.1 = (bf16[256,4096]{1,0:T(8,128)(2,1)S(1)}, f32[8,256,512]{2,1,0:T(8,128)S(1)}, bf16[2,8,128,512]{3,2,1,0:T(8,128)(2,1)S(1)}) custom-call(bf16[256,4096]{1,0:T(8,128)(2,1)} %x_ref.1, bf16[4096,2560]{1,0:T(8,128)(2,1)} %wg_ref.1, bf16[4096,2560]{1,0:T(8,128)(2,1)} %wu_ref.1, bf16[2560,4096]{1,0:T(8,128)(2,1)} %wd_ref.1), custom_call_target="tpu_custom_call" | custom-call | flops 64424509440 | bytes 251658240 | tf_op jit(solution)/shard_map/mlp_ring/pallas_call | solution.py:242
  139.6 1.3 finish.1
